TPU v7x, 1024 devices: a whole 8x8x8 slice. The times are simulated.
1024 devices in a mesh: gx: 16 (over x, core), gy: 8 (over y), gz: 8 (over z).
Axes of the slice: x: 8, y: 8, z: 8, core: 2. Of those that a mesh axis runs over, the one named last changes fastest.
Arguments:
- coarse_pdfs: float32 [19, 64, 32, 512], P(None, 'gx', 'gy', 'gz'), may hold values from 0.1 to 32
- fine_pdfs: float32 [19, 64, 64, 1024], P(None, 'gx', 'gy', 'gz'), may hold values from 0.1 to 32
- centers: int32 [3, 3, 4, 4, 16], replicated, may hold values from 4 to 59, as said below
- sphere_velocity: float32 [3, 4, 4, 16], replicated, may hold values from -0.05 to 0.05
Outputs:
- coarse_next: float32 [19, 64, 32, 512], P(None, 'gx', 'gy', 'gz')
- fine_next: float32 [19, 64, 64, 1024], P(None, 'gx', 'gy', 'gz')
- sphere_force: float32 [2, 3, 4, 4, 16], replicated
Inputs may be any that keep to these rules, and one draw needn't show every extreme that they name: `centers`: each coordinate of a center is counted from its box's first cell; from one substep to the next it changes by -1, 0 or 1, and the same change repeats in the second substep.
All inputs are finite; a program needn't handle non-finite values.
Results may differ from a plain program's by a relative error of at most 0.0003.
Values sent between devices are 32-bit elements; how exact they have to be, the bound alone decides.
No kernel may reach another device: no remote copies, remote signals or barrier semaphores. Data moves between devices by JAX's collectives and lax.ppermute only.
A program may use at most 32 MiB of HBM per device.

v0:
```python
import jax
import jax.numpy as jnp
from jax import lax
from jax.sharding import Mesh
from jax.sharding import PartitionSpec as P

BOX_XY = 16
BOX_Z = 64
RADIUS = 4
GX_GY_GZ = ("gx_0", "gx_1", "gy", "gz")
GX = ("gx_0", "gx_1")


VELOCITIES = (
    (0, 0, 0),
    (1, 0, 0),
    (-1, 0, 0),
    (0, 1, 0),
    (0, -1, 0),
    (0, 0, 1),
    (0, 0, -1),
    (1, 1, 0),
    (-1, -1, 0),
    (1, -1, 0),
    (-1, 1, 0),
    (1, 0, 1),
    (-1, 0, -1),
    (1, 0, -1),
    (-1, 0, 1),
    (0, 1, 1),
    (0, -1, -1),
    (0, 1, -1),
    (0, -1, 1),
)
OPPOSITE = (0, 2, 1, 4, 3, 6, 5, 8, 7, 10, 9, 12, 11, 14, 13, 16, 15, 18, 17)
WEIGHTS = (1.0 / 3.0,) + (1.0 / 18.0,) * 6 + (1.0 / 36.0,) * 12
COARSE_RATE = 1.25
FINE_RATE = 1.0 / 1.1
HIGHEST = lax.Precision.HIGHEST


def over_axes(x, axes):
    for axis in axes:
        x = lax.psum(x, axis)
    return x


def extended(cells, sides, width):
    for axis, dim in sides:
        count = lax.axis_size(axis)
        head = lax.slice_in_dim(cells, 0, width, axis=dim)
        tail = lax.slice_in_dim(cells, cells.shape[dim] - width, cells.shape[dim], axis=dim)
        cells = jnp.concatenate(
            [
                lax.ppermute(tail, axis, [(i, (i + 1) % count) for i in range(count)]),
                cells,
                lax.ppermute(head, axis, [((i + 1) % count, i) for i in range(count)]),
            ],
            axis=dim,
        )
    return cells


def project(vectors, direction):
    projected = jnp.zeros_like(vectors[0])
    for dimension in range(3):
        sign = VELOCITIES[direction][dimension]
        if sign == 1:
            projected = projected + vectors[dimension]
        elif sign == -1:
            projected = projected - vectors[dimension]
    return projected


def speed_squared(vectors):
    return vectors[0] * vectors[0] + vectors[1] * vectors[1] + vectors[2] * vectors[2]


def equilibrium(density, vectors, speed_sq, direction):
    projected = project(vectors, direction)
    return (
        WEIGHTS[direction]
        * density
        * (1.0 + 3.0 * projected + 4.5 * projected * projected - 1.5 * speed_sq)
    )


def total_density(populations):
    density = populations[0]
    for direction in range(1, 19):
        density = density + populations[direction]
    return density


def collide(populations, relaxation):
    density = total_density(populations)
    velocity = []
    for dimension in range(3):
        summed = jnp.zeros_like(density)
        for direction in range(19):
            sign = VELOCITIES[direction][dimension]
            if sign == 1:
                summed = summed + populations[direction]
            elif sign == -1:
                summed = summed - populations[direction]
        velocity.append(summed / density)
    speed_sq = speed_squared(velocity)
    relaxed = []
    for direction in range(19):
        target = equilibrium(density, velocity, speed_sq, direction)
        relaxed.append(populations[direction] - relaxation * (populations[direction] - target))
    return jnp.stack(relaxed)


def box_onehot(coords, box_size, box_count):
    box_index = jnp.floor_divide(coords, box_size)
    onehot = (box_index[None, :] == jnp.arange(box_count, dtype=jnp.int32)[:, None]).astype(
        jnp.float32
    )
    offsets = (coords - box_index * box_size).astype(jnp.float32)
    return (onehot, offsets)


def geometry(coord_x, coord_y, coord_z, centers, sphere_velocity):
    count_x, count_y, count_z = (centers.shape[2], centers.shape[3], centers.shape[4])
    table_x, offset_x = box_onehot(coord_x, BOX_XY, count_x)
    table_y, offset_y = box_onehot(coord_y, BOX_XY, count_y)
    table_z, offset_z = box_onehot(coord_z, BOX_Z, count_z)
    inside = ((coord_x >= 0) & (coord_x < count_x * BOX_XY))[:, None, None]

    def spread(values):
        return jnp.einsum("abc,ax,by,cz->xyz", values, table_x, table_y, table_z, precision=HIGHEST)

    solids = []
    for moment in range(3):
        gap_x = offset_x[:, None, None] - spread(centers[moment, 0].astype(jnp.float32))
        gap_y = offset_y[None, :, None] - spread(centers[moment, 1].astype(jnp.float32))
        gap_z = offset_z[None, None, :] - spread(centers[moment, 2].astype(jnp.float32))
        distance = gap_x * gap_x + gap_y * gap_y + gap_z * gap_z
        solids.append((distance <= float(RADIUS * RADIUS)) & inside)
    velocity_field = [spread(sphere_velocity[dimension]) for dimension in range(3)]
    return (solids, velocity_field, (table_x, table_y, table_z))


def pull_from(values, direction):
    step_x, step_y, step_z = VELOCITIES[direction]
    width_x = values.shape[-3] - 2
    width_y = values.shape[-2] - 2
    width_z = values.shape[-1] - 2
    return values[
        ...,
        1 - step_x : 1 - step_x + width_x,
        1 - step_y : 1 - step_y + width_y,
        1 - step_z : 1 - step_z + width_z,
    ]


def trimmed(values, width):
    trim_by = 2 - width
    return values[..., trim_by:-trim_by, trim_by:-trim_by, trim_by:-trim_by]


def upsample(ghost_plane):
    return jnp.repeat(jnp.repeat(ghost_plane, 2, axis=1), 2, axis=2)


def coalesce(ghost_plane):
    grouped = ghost_plane.reshape(19, ghost_plane.shape[1] // 2, 2, ghost_plane.shape[2] // 2, 2)
    return (
        grouped[:, :, 0, :, 0]
        + grouped[:, :, 1, :, 0]
        + grouped[:, :, 0, :, 1]
        + grouped[:, :, 1, :, 1]
    ) * 0.25


def substep(padded, solid_prev, solid_new, velocity_field, margin, tables):
    interior = padded[:, 1:-1, 1:-1, 1:-1]
    size_x = interior.shape[1] - 2 * margin
    size_y = interior.shape[2] - 2 * margin
    size_z = interior.shape[3] - 2 * margin
    density = total_density(padded)
    density_in = density[1:-1, 1:-1, 1:-1]
    open_cells = jnp.logical_not(solid_prev) & jnp.logical_not(solid_new)
    moving = open_cells[1:-1, 1:-1, 1:-1]
    numerator = WEIGHTS[0] * density_in
    denominator = jnp.full(density_in.shape, WEIGHTS[0], jnp.float32)
    arrived = [interior[0]]
    push_sums = [
        jnp.zeros((size_x + 2, size_y + 2, size_z + 2), jnp.float32) for dimension in range(3)
    ]
    for direction in range(1, 19):
        step_x, step_y, step_z = VELOCITIES[direction]
        solid_next = pull_from(solid_new, direction)
        neighbour_velocity = [pull_from(values, direction) for values in velocity_field]
        returned = interior[OPPOSITE[direction]]
        bounced = returned + 6.0 * WEIGHTS[direction] * density_in * project(
            neighbour_velocity, direction
        )
        arrived.append(jnp.where(solid_next, bounced, pull_from(padded[direction], direction)))
        link_term = jnp.where(solid_next & moving, returned + bounced, 0.0)
        own_term = link_term[
            margin : margin + size_x, margin : margin + size_y, margin : margin + size_z
        ]
        padded_term = jnp.pad(own_term, 2)
        pushed = padded_term[
            1 + step_x : 3 + step_x + size_x,
            1 + step_y : 3 + step_y + size_y,
            1 + step_z : 3 + step_z + size_z,
        ]
        for dimension in range(3):
            sign = VELOCITIES[direction][dimension]
            if sign == 1:
                push_sums[dimension] = push_sums[dimension] - pushed
            elif sign == -1:
                push_sums[dimension] = push_sums[dimension] + pushed
        open_next = pull_from(open_cells, direction).astype(jnp.float32)
        numerator = numerator + WEIGHTS[direction] * pull_from(density, direction) * open_next
        denominator = denominator + WEIGHTS[direction] * open_next
    refill_density = numerator / denominator
    own_velocity = [values[1:-1, 1:-1, 1:-1] for values in velocity_field]
    speed_sq = speed_squared(own_velocity)
    covered = solid_new[1:-1, 1:-1, 1:-1]
    uncovered = solid_prev[1:-1, 1:-1, 1:-1]
    updated = []
    for direction in range(19):
        refill = equilibrium(refill_density, own_velocity, speed_sq, direction)
        updated.append(
            jnp.where(
                covered, interior[direction], jnp.where(uncovered, refill, arrived[direction])
            )
        )
    table_x, table_y, table_z = tables
    forces = jnp.einsum(
        "kxyz,ax,by,cz->kabc", jnp.stack(push_sums), table_x, table_y, table_z, precision=HIGHEST
    )
    return (jnp.stack(updated), forces)


def reduce_forces(forces):
    return over_axes(forces, GX_GY_GZ)


def shards(coarse_pdfs, fine_pdfs, centers, sphere_velocity):
    own_x, own_y, own_z = (fine_pdfs.shape[1], fine_pdfs.shape[2], fine_pdfs.shape[3])
    coarse_x = coarse_pdfs.shape[1]
    devices_x = lax.axis_size(GX)
    index_x = lax.axis_index(GX)
    total_x = own_x * devices_x
    total_y = own_y * lax.axis_size("gy")
    total_z = own_z * lax.axis_size("gz")
    coord_x = index_x * own_x + jnp.arange(-2, own_x + 2, dtype=jnp.int32)
    coord_y = (lax.axis_index("gy") * own_y + jnp.arange(-2, own_y + 2, dtype=jnp.int32)) % total_y
    coord_z = (lax.axis_index("gz") * own_z + jnp.arange(-2, own_z + 2, dtype=jnp.int32)) % total_z
    solids, velocity_field, tables = geometry(coord_x, coord_y, coord_z, centers, sphere_velocity)
    narrow_tables = (tables[0][:, 1:-1], tables[1][:, 1:-1], tables[2][:, 1:-1])
    narrow_velocity = [trimmed(values, 1) for values in velocity_field]
    coarse_post = collide(coarse_pdfs, COARSE_RATE)
    coarse_padded = extended(coarse_post, ((GX, 1), ("gy", 2), ("gz", 3)), 1)
    left_fill = upsample(coarse_padded[:, 0])
    right_fill = upsample(coarse_padded[:, coarse_x + 1])

    def with_explosion(fresh, width):
        trim_by = 2 - width
        span_x = coord_x.shape[0] - 2 * trim_by
        part_x = coord_x[trim_by : trim_by + span_x]
        left_part = left_fill[
            :, trim_by : left_fill.shape[1] - trim_by, trim_by : left_fill.shape[2] - trim_by
        ]
        right_part = right_fill[
            :, trim_by : right_fill.shape[1] - trim_by, trim_by : right_fill.shape[2] - trim_by
        ]
        is_left = (part_x < 0)[None, :, None, None]
        is_right = (part_x >= total_x)[None, :, None, None]
        return jnp.where(
            is_left, left_part[:, None], jnp.where(is_right, right_part[:, None], fresh)
        )

    widened = extended(fine_pdfs, ((GX, 1), ("gy", 2), ("gz", 3)), 2)
    first_post = collide(widened, FINE_RATE)
    middle, first_forces = substep(
        with_explosion(first_post, 2), solids[0], solids[1], velocity_field, 1, narrow_tables
    )
    second_padded = with_explosion(collide(middle, FINE_RATE), 1)
    fine_next, second_forces = substep(
        second_padded,
        trimmed(solids[1], 1),
        trimmed(solids[2], 1),
        narrow_velocity,
        0,
        narrow_tables,
    )
    left_coal = coalesce(first_post[:, 1])
    right_coal = coalesce(first_post[:, own_x + 2])
    ghost_x = jnp.arange(coarse_x + 2, dtype=jnp.int32)
    left_ghost = ((ghost_x == 0) & (index_x == 0))[None, :, None, None]
    right_ghost = ((ghost_x == coarse_x + 1) & (index_x == devices_x - 1))[None, :, None, None]
    coarse_ready = jnp.where(
        left_ghost, left_coal[:, None], jnp.where(right_ghost, right_coal[:, None], coarse_padded)
    )
    coarse_next = jnp.stack(
        [pull_from(coarse_ready[direction], direction) for direction in range(19)]
    )
    sphere_force = jnp.stack([reduce_forces(first_forces), reduce_forces(second_forces)])
    return (coarse_next, fine_next, sphere_force)


def solution(mesh):
    split = Mesh(
        mesh.devices.reshape(8, 2, mesh.shape["gy"], mesh.shape["gz"]), ("gx_0", "gx_1", "gy", "gz")
    )
    return jax.shard_map(
        shards,
        mesh=split,
        in_specs=(P(None, GX, "gy", "gz"), P(None, GX, "gy", "gz"), P(), P()),
        out_specs=(P(None, GX, "gy", "gz"), P(None, GX, "gy", "gz"), P()),
        check_vma=False,
    )
```

profile of v0, /device:TPU:16, one launch (start us, length us, event | category | flops | bytes accessed | tf_op | source)
XLA Modules:
  0.0 221.2 jit_solution(4525208728560230803)
XLA Ops:
  0.6 1.1 copy.64
  1.9 2.3 %collective-permute-start.1 = (f32[19,2,8,128]{3,1,2,0:T(2,128)S(1)}, f32[19,2,8,128]{3,1,2,0:T(2,128)S(1)}, u32[]{:S(2)}, u32[]{:S(2)}) collective-permute-start(f32[19,2,8,128]{3,1,2,0:T(2,128)S(1)} %get-tuple-element.220), channel_id=1, source_target_pairs={{64,0},{128,64},{192,128},{256,192},{320,256},{384,320},{448,384},... | collective-permute-start | bytes 466952 | tf_op jit(solution)/shard_map/ppermute | solution.py:57
  4.2 0.9 constant_dynamic-update-slice_fusion.37
  5.1 0.7 constant_dynamic-update-slice_fusion.36
  5.8 0.7 constant_dynamic-update-slice_fusion.35
  6.6 0.7 constant_dynamic-update-slice_fusion.34
  7.3 0.7 constant_dynamic-update-slice_fusion.33
  8.0 0.7 constant_dynamic-update-slice_fusion.32
  8.7 0.7 constant_dynamic-update-slice_fusion.31
  9.4 0.7 constant_dynamic-update-slice_fusion.30
  10.2 0.7 constant_dynamic-update-slice_fusion.29
  10.9 0.7 constant_dynamic-update-slice_fusion.28
  11.6 0.7 constant_dynamic-update-slice_fusion.27
  12.3 0.7 constant_dynamic-update-slice_fusion.26
  13.0 0.7 constant_dynamic-update-slice_fusion.25
  13.8 0.7 constant_dynamic-update-slice_fusion.24
  14.5 0.7 constant_dynamic-update-slice_fusion.23
  15.2 0.7 constant_dynamic-update-slice_fusion.22
  15.9 0.7 constant_dynamic-update-slice_fusion.21
  16.6 0.7 constant_dynamic-update-slice_fusion.20
  17.4 0.7 constant_dynamic-update-slice_fusion.19
  18.1 3.0 %collective-permute-start.7 = (f32[19,1,4,64]{3,2,1,0:T(4,128)S(1)}, f32[19,1,4,64]{3,2,1,0:T(4,128)S(1)}, u32[]{:S(2)}, u32[]{:S(2)}) collective-permute-start(f32[19,1,4,64]{3,2,1,0:T(4,128)S(1)} %get-tuple-element.224), channel_id=1, source_target_pairs={{64,0},{128,64},{192,128},{256,192},{320,256},{384,320},{448,384},... | collective-permute-start | bytes 58376 | tf_op jit(solution)/shard_map/ppermute | solution.py:57
  29.4 1.0 not_and_fusion
  30.5 1.1 fusion.1003
  32.2 12.6 %collective-permute-start.9 = (f32[19,6,1,64]{3,2,1,0:T(1,128)S(1)}, f32[19,6,1,64]{3,2,1,0:T(1,128)S(1)}, u32[]{:S(2)}, u32[]{:S(2)}) collective-permute-start(f32[19,6,1,64]{3,2,1,0:T(1,128)S(1)} %get-tuple-element.222), channel_id=1, source_target_pairs={{8,0},{16,8},{24,16},{32,24},{40,32},{48,40},{56,48},{0,56},{9,1},... | collective-permute-start | bytes 87560 | tf_op jit(solution)/shard_map/ppermute | solution.py:57
  44.8 1.9 collective-permute-start.8
  46.9 3.9 %collective-permute-start.3 = (f32[19,8,2,128]{3,1,2,0:T(8,128)S(1)}, f32[19,8,2,128]{3,1,2,0:T(8,128)S(1)}, u32[]{:S(2)}, u32[]{:S(2)}) collective-permute-start(f32[19,8,2,128]{3,1,2,0:T(8,128)S(1)} %get-tuple-element.195), channel_id=1, source_target_pairs={{8,0},{16,8},{24,16},{32,24},{40,32},{48,40},{56,48},{0,56},{9,1},... | collective-permute-start | bytes 466952 | tf_op jit(solution)/shard_map/ppermute | solution.py:57
  50.8 1.9 collective-permute-start.2
  53.3 0.7 slice.2318
  54.2 0.7 slice.2547
  55.2 2.8 %collective-permute-done.2 = f32[19,8,2,128]{3,1,2,0:T(8,128)S(1)} collective-permute-done((f32[19,8,2,128]{3,1,2,0:T(8,128)S(1)}, f32[19,8,2,128]{3,1,2,0:T(8,128)S(1)}, u32[]{:S(2)}, u32[]{:S(2)}) %collective-permute-start.2) | collective-permute-done | bytes 155680 | tf_op jit(solution)/shard_map/ppermute | solution.py:55
  59.2 1.4 copy.68
  60.6 10.4 %collective-permute-start.5 = (f32[19,8,12,2]{0,1,3,2:T(8,128)}, f32[19,8,12,2]{0,1,3,2:T(8,128)S(1)}, u32[]{:S(2)}, u32[]{:S(2)}) collective-permute-start(f32[19,8,12,2]{0,1,3,2:T(8,128)} %copy.68), channel_id=1, source_target_pairs={{1,0},{2,1},{3,2},{4,3},{5,4},{6,5},{7,6},{0,7},{9,8},{10,9},{11,1... | collective-permute-start | bytes 43784 | tf_op jit(solution)/shard_map/ppermute | solution.py:57
  71.0 0.7 copy.67
  71.8 2.1 collective-permute-start.4
  73.8 1.1 fusion.1000
  74.9 5.1 %collective-permute-start.11 = (f32[19,6,6,1]{3,2,1,0:T(8,128)}, f32[19,6,6,1]{3,2,1,0:T(8,128)}, u32[]{:S(2)}, u32[]{:S(2)}) collective-permute-start(f32[19,6,6,1]{3,2,1,0:T(8,128)} %get-tuple-element.218), channel_id=1, source_target_pairs={{1,0},{2,1},{3,2},{4,3},{5,4},{6,5},{7,6},{0,7},{9,8},{10,9},{11,1... | collective-permute-start | bytes 8216 | tf_op jit(solution)/shard_map/ppermute | solution.py:57
  80.0 2.1 collective-permute-start.10
  82.1 1.0 copy.70
  83.1 1.9 copy.69
  85.0 1.4 pad_maximum_fusion
  88.1 0.9 copy-done.2
  92.0 2.5 %select_select_fusion.2 = (f32[19,6,6,66]{3,2,1,0:T(8,128)}, f32[19,6,6,66]{3,2,1,0:T(8,128)S(1)}) fusion(f32[19,6,66]{2,1,0:T(8,128)S(1)} %bitcast.1055, f32[19,6,66]{2,1,0:T(8,128)S(1)} %bitcast.1056, pred[6]{0:T(512)(128)(4,1)S(1)} %copy-done.38, pred[6]{0:T(512)(128)(4,1)S(1)} %copy-done.39, f32[19,6,6,1]{3,2,1,0:T(8,128)} %collective-permute-done.11, ...), kind=kLoop, calls=%fused_computation.8 | loop fusion | flops 361152 | bytes 601932 | tf_op jit(solution)/shard_map/jit(_where)/select_n | solution.py:298
  95.6 0.7 copy.100
  97.4 1.4 copy.99
  98.7 2.0 select_select_fusion
  100.8 1.2 slice_bitcast_fusion
  102.1 0.9 slice.2254
  103.0 0.9 slice.2252
  104.3 1.4 copy.89
  105.7 2.0 copy.87
  107.9 0.8 select_select_fusion.3
  109.2 1.7 constant_dynamic-update-slice_fusion.75
  117.7 0.7 copy.123
  119.3 0.9 fusion.658
  120.2 1.0 fusion.675
  121.2 1.0 fusion.664
  122.1 1.0 fusion.660
  123.2 1.0 fusion.674
  125.9 32.5 %all-reduce.38 = (f32[3,4,4,16]{3,1,0,2:T(4,128)S(1)}, f32[3,4,4,16]{3,1,0,2:T(4,128)S(1)}) all-reduce(f32[3,4,4,16]{3,1,0,2:T(4,128)S(1)} %convolution_bitcast_fusion, f32[3,4,4,16]{3,1,0,2:T(4,128)S(1)} %convolution_bitcast_fusion.1), channel_id=1, replica_groups=mesh['gx_0'=8,'gx_1'=2,'gy'=8,'gz'=8] {'gx_0'}, use_global_device_ids=true, to_apply=%region_4.5 | all-reduce | flops 1536 | bytes 12288 | tf_op jit(solution)/shard_map/psum | solution.py:44
  158.4 3.5 %all-reduce.39 = (f32[3,4,4,16]{3,1,0,2:T(4,128)S(1)}, f32[3,4,4,16]{3,1,0,2:T(4,128)S(1)}) all-reduce(f32[3,4,4,16]{3,1,0,2:T(4,128)S(1)} %get-tuple-element.19, f32[3,4,4,16]{3,1,0,2:T(4,128)S(1)} %get-tuple-element.20), channel_id=1, replica_groups=mesh['gx_0'=8,'gx_1'=2,'gy'=8,'gz'=8] {'gx_1'}, use_global_device_ids=true, to_apply=%region_5.6 | all-reduce | flops 1536 | bytes 12288 | tf_op jit(solution)/shard_map/psum | solution.py:44
  161.9 29.4 %all-reduce.37 = (f32[3,4,4,16]{3,1,0,2:T(4,128)S(1)}, f32[3,4,4,16]{3,1,0,2:T(4,128)S(1)}) all-reduce(f32[3,4,4,16]{3,1,0,2:T(4,128)S(1)} %get-tuple-element.21, f32[3,4,4,16]{3,1,0,2:T(4,128)S(1)} %get-tuple-element.22), channel_id=1, replica_groups=mesh['gx_0'=8,'gx_1'=2,'gy'=8,'gz'=8] {'gy'}, use_global_device_ids=true, to_apply=%region_6.7 | all-reduce | flops 1536 | bytes 12288 | tf_op jit(solution)/shard_map/psum | solution.py:44
  191.3 27.4 %all-reduce.36 = (f32[1,3,4,4,16]{4,2,1,3,0:T(4,128)S(1)}, f32[1,3,4,4,16]{4,2,1,3,0:T(4,128)S(1)}) all-reduce(f32[1,3,4,4,16]{4,2,1,3,0:T(4,128)S(1)} %bitcast.1057, f32[1,3,4,4,16]{4,2,1,3,0:T(4,128)S(1)} %bitcast.1058), channel_id=1, replica_groups=mesh['gx_0'=8,'gx_1'=2,'gy'=8,'gz'=8] {'gz'}, use_global_device_ids=true, to_apply=%region_7.8 | all-reduce | flops 1536 | bytes 12288 | tf_op jit(solution)/shard_map/psum | solution.py:44
  220.5 0.7 copy-done.44
  (282 shorter events, 29.8 us)
Async XLA Ops:
  0.6 20.5 %copy-start.36 = (s32[3,3,4,4,16]{4,3,2,1,0:T(4,128)S(1)}, s32[3,3,4,4,16]{4,3,2,1,0:T(4,128)}, u32[]{:S(2)}) copy-start(s32[3,3,4,4,16]{4,3,2,1,0:T(4,128)} %param.6) | copy-start | bytes 27652
  1.7 23.2 %copy-start.37 = (f32[3,4,4,16]{3,2,1,0:T(4,128)S(1)}, f32[3,4,4,16]{3,2,1,0:T(4,128)}, u32[]{:S(2)}) copy-start(f32[3,4,4,16]{3,2,1,0:T(4,128)} %param.7) | copy-start | bytes 9220
  1.9 44.9 %collective-permute-start.1 = (f32[19,2,8,128]{3,1,2,0:T(2,128)S(1)}, f32[19,2,8,128]{3,1,2,0:T(2,128)S(1)}, u32[]{:S(2)}, u32[]{:S(2)}) collective-permute-start(f32[19,2,8,128]{3,1,2,0:T(2,128)S(1)} %get-tuple-element.220), channel_id=1, source_target_pairs={{64,0},{128,64},{192,128},{256,192},{320,256},{384,320},{448,384},... | collective-permute-start | bytes 466952 | tf_op jit(solution)/shard_map/ppermute | solution.py:57
  4.2 42.6 %collective-permute-start = (f32[19,2,8,128]{3,1,2,0:T(2,128)S(1)}, f32[19,2,8,128]{3,1,2,0:T(2,128)S(1)}, u32[]{:S(2)}, u32[]{:S(2)}) collective-permute-start(f32[19,2,8,128]{3,1,2,0:T(2,128)S(1)} %get-tuple-element.219), channel_id=1, source_target_pairs={{0,64},{64,128},{128,192},{192,256},{256,320},{320,384},{384,448},... | collective-permute-start | bytes 466952 | tf_op jit(solution)/shard_map/ppermute | solution.py:55
  18.1 14.0 %collective-permute-start.7 = (f32[19,1,4,64]{3,2,1,0:T(4,128)S(1)}, f32[19,1,4,64]{3,2,1,0:T(4,128)S(1)}, u32[]{:S(2)}, u32[]{:S(2)}) collective-permute-start(f32[19,1,4,64]{3,2,1,0:T(4,128)S(1)} %get-tuple-element.224), channel_id=1, source_target_pairs={{64,0},{128,64},{192,128},{256,192},{320,256},{384,320},{448,384},... | collective-permute-start | bytes 58376 | tf_op jit(solution)/shard_map/ppermute | solution.py:57
  21.1 11.1 %collective-permute-start.6 = (f32[19,1,4,64]{3,2,1,0:T(4,128)S(1)}, f32[19,1,4,64]{3,2,1,0:T(4,128)S(1)}, u32[]{:S(2)}, u32[]{:S(2)}) collective-permute-start(f32[19,1,4,64]{3,2,1,0:T(4,128)S(1)} %get-tuple-element.223), channel_id=1, source_target_pairs={{0,64},{64,128},{128,192},{192,256},{256,320},{320,384},{384,448},... | collective-permute-start | bytes 58376 | tf_op jit(solution)/shard_map/ppermute | solution.py:55
  32.1 25.8 %copy-start.10 = (f32[19,1,4,64]{3,2,1,0:T(4,128)}, f32[19,1,4,64]{3,2,1,0:T(4,128)S(1)}, u32[]{:S(2)}) copy-start(f32[19,1,4,64]{3,2,1,0:T(4,128)S(1)} %collective-permute-done.6) | copy-start | bytes 58372
  32.2 22.7 %collective-permute-start.9 = (f32[19,6,1,64]{3,2,1,0:T(1,128)S(1)}, f32[19,6,1,64]{3,2,1,0:T(1,128)S(1)}, u32[]{:S(2)}, u32[]{:S(2)}) collective-permute-start(f32[19,6,1,64]{3,2,1,0:T(1,128)S(1)} %get-tuple-element.222), channel_id=1, source_target_pairs={{8,0},{16,8},{24,16},{32,24},{40,32},{48,40},{56,48},{0,56},{9,1},... | collective-permute-start | bytes 87560 | tf_op jit(solution)/shard_map/ppermute | solution.py:57
  44.8 10.1 %collective-permute-start.8 = (f32[19,6,1,64]{3,2,1,0:T(1,128)S(1)}, f32[19,6,1,64]{3,2,1,0:T(1,128)S(1)}, u32[]{:S(2)}, u32[]{:S(2)}) collective-permute-start(f32[19,6,1,64]{3,2,1,0:T(1,128)S(1)} %get-tuple-element.221), channel_id=1, source_target_pairs={{0,8},{8,16},{16,24},{24,32},{32,40},{40,48},{48,56},{56,0},{1,9},... | collective-permute-start | bytes 87560 | tf_op jit(solution)/shard_map/ppermute | solution.py:55
  46.9 8.3 %collective-permute-start.3 = (f32[19,8,2,128]{3,1,2,0:T(8,128)S(1)}, f32[19,8,2,128]{3,1,2,0:T(8,128)S(1)}, u32[]{:S(2)}, u32[]{:S(2)}) collective-permute-start(f32[19,8,2,128]{3,1,2,0:T(8,128)S(1)} %get-tuple-element.195), channel_id=1, source_target_pairs={{8,0},{16,8},{24,16},{32,24},{40,32},{48,40},{56,48},{0,56},{9,1},... | collective-permute-start | bytes 466952 | tf_op jit(solution)/shard_map/ppermute | solution.py:57
  50.8 7.1 %collective-permute-start.2 = (f32[19,8,2,128]{3,1,2,0:T(8,128)S(1)}, f32[19,8,2,128]{3,1,2,0:T(8,128)S(1)}, u32[]{:S(2)}, u32[]{:S(2)}) collective-permute-start(f32[19,8,2,128]{3,1,2,0:T(8,128)S(1)} %get-tuple-element.194), channel_id=1, source_target_pairs={{0,8},{8,16},{16,24},{24,32},{32,40},{40,48},{48,56},{56,0},{1,9},... | collective-permute-start | bytes 466952 | tf_op jit(solution)/shard_map/ppermute | solution.py:55
  54.9 3.0 %copy-start.30 = (f32[19,6,1,64]{3,2,1,0:T(1,128)}, f32[19,6,1,64]{3,2,1,0:T(1,128)S(1)}, u32[]{:S(2)}) copy-start(f32[19,6,1,64]{3,2,1,0:T(1,128)S(1)} %collective-permute-done.9) | copy-start | bytes 87556
  54.9 3.0 %copy-start.32 = (f32[19,6,1,64]{3,2,1,0:T(1,128)}, f32[19,6,1,64]{3,2,1,0:T(1,128)S(1)}, u32[]{:S(2)}) copy-start(f32[19,6,1,64]{3,2,1,0:T(1,128)S(1)} %collective-permute-done.8) | copy-start | bytes 87556
  55.2 2.8 %copy-start.6 = (f32[19,8,2,128]{3,1,2,0:T(8,128)}, f32[19,8,2,128]{3,1,2,0:T(8,128)S(1)}, u32[]{:S(2)}) copy-start(f32[19,8,2,128]{3,1,2,0:T(8,128)S(1)} %collective-permute-done.3) | copy-start | bytes 466948
  58.0 0.7 copy-start.8
  60.6 21.6 %collective-permute-start.5 = (f32[19,8,12,2]{0,1,3,2:T(8,128)}, f32[19,8,12,2]{0,1,3,2:T(8,128)S(1)}, u32[]{:S(2)}, u32[]{:S(2)}) collective-permute-start(f32[19,8,12,2]{0,1,3,2:T(8,128)} %copy.68), channel_id=1, source_target_pairs={{1,0},{2,1},{3,2},{4,3},{5,4},{6,5},{7,6},{0,7},{9,8},{10,9},{11,1... | collective-permute-start | bytes 43784 | tf_op jit(solution)/shard_map/ppermute | solution.py:57
  71.7 13.2 %copy-start.7 = (f32[19,8,2,128]{3,1,2,0:T(8,128)S(1)}, f32[19,8,2,128]{3,1,2,0:T(8,128)}, u32[]{:S(2)}) copy-start(f32[19,8,2,128]{3,1,2,0:T(8,128)} %copy-done.6) | copy-start | bytes 466948
  71.7 13.3 %copy-start.9 = (f32[19,8,2,128]{3,1,2,0:T(8,128)S(1)}, f32[19,8,2,128]{3,1,2,0:T(8,128)}, u32[]{:S(2)}) copy-start(f32[19,8,2,128]{3,1,2,0:T(8,128)} %copy-done.8) | copy-start | bytes 466948
  71.8 11.3 %collective-permute-start.4 = (f32[19,8,12,2]{0,1,3,2:T(8,128)S(1)}, f32[19,8,12,2]{0,1,3,2:T(8,128)}, u32[]{:S(2)}, u32[]{:S(2)}) collective-permute-start(f32[19,8,12,2]{0,1,3,2:T(8,128)S(1)} %copy.67), channel_id=1, source_target_pairs={{0,1},{1,2},{2,3},{3,4},{4,5},{5,6},{6,7},{7,0},{8,9},{9,10},{10,1... | collective-permute-start | bytes 43784 | tf_op jit(solution)/shard_map/ppermute | solution.py:55
  74.9 17.0 %collective-permute-start.11 = (f32[19,6,6,1]{3,2,1,0:T(8,128)}, f32[19,6,6,1]{3,2,1,0:T(8,128)}, u32[]{:S(2)}, u32[]{:S(2)}) collective-permute-start(f32[19,6,6,1]{3,2,1,0:T(8,128)} %get-tuple-element.218), channel_id=1, source_target_pairs={{1,0},{2,1},{3,2},{4,3},{5,4},{6,5},{7,6},{0,7},{9,8},{10,9},{11,1... | collective-permute-start | bytes 8216 | tf_op jit(solution)/shard_map/ppermute | solution.py:57
  80.0 12.0 %collective-permute-start.10 = (f32[19,6,6,1]{3,2,1,0:T(8,128)}, f32[19,6,6,1]{3,2,1,0:T(8,128)}, u32[]{:S(2)}, u32[]{:S(2)}) collective-permute-start(f32[19,6,6,1]{3,2,1,0:T(8,128)} %get-tuple-element.217), channel_id=1, source_target_pairs={{0,1},{1,2},{2,3},{3,4},{4,5},{5,6},{6,7},{7,0},{8,9},{9,10},{10,1... | collective-permute-start | bytes 8216 | tf_op jit(solution)/shard_map/ppermute | solution.py:55
  87.7 1.2 copy-start.2
  90.6 1.4 copy-start.11
  90.6 1.4 copy-start.31
  90.6 1.4 copy-start.33
  90.6 1.4 copy-start.38
  90.6 1.4 copy-start.39
  96.5 2.3 %copy-start.42 = (pred[8]{0:T(512)(128)(4,1)S(1)}, pred[8]{0:T(512)(128)(4,1)}, u32[]{:S(2)}) copy-start(pred[8]{0:T(512)(128)(4,1)} %get-tuple-element.279) | copy-start | bytes 28
  96.5 2.3 %copy-start.43 = (pred[8]{0:T(512)(128)(4,1)S(1)}, pred[8]{0:T(512)(128)(4,1)}, u32[]{:S(2)}) copy-start(pred[8]{0:T(512)(128)(4,1)} %get-tuple-element.280) | copy-start | bytes 28
  97.4 1.4 copy-start
  100.8 2.1 copy-start.1
  103.0 1.4 copy-start.3
  103.0 4.9 %copy-start.34 = (pred[8,12,132]{2,0,1:T(8,128)(4,1)S(1)}, pred[8,12,132]{2,0,1:T(8,128)(4,1)}, u32[]{:S(2)}) copy-start(pred[8,12,132]{2,0,1:T(8,128)(4,1)} %get-tuple-element.96) | copy-start | bytes 38020
  105.7 3.0 %copy-start.12 = (f32[8,12,132]{2,0,1:T(8,128)S(1)}, f32[8,12,132]{2,0,1:T(8,128)}, u32[]{:S(2)}) copy-start(f32[8,12,132]{2,0,1:T(8,128)} %get-tuple-element.142) | copy-start | bytes 152068
  105.7 3.0 %copy-start.13 = (f32[8,12,132]{2,0,1:T(8,128)S(1)}, f32[8,12,132]{2,0,1:T(8,128)}, u32[]{:S(2)}) copy-start(f32[8,12,132]{2,0,1:T(8,128)} %get-tuple-element.143) | copy-start | bytes 152068
  105.7 3.0 %copy-start.14 = (f32[8,12,132]{2,0,1:T(8,128)S(1)}, f32[8,12,132]{2,0,1:T(8,128)}, u32[]{:S(2)}) copy-start(f32[8,12,132]{2,0,1:T(8,128)} %get-tuple-element.144) | copy-start | bytes 152068
  105.7 3.0 %copy-start.15 = (f32[8,12,132]{2,0,1:T(8,128)S(1)}, f32[8,12,132]{2,0,1:T(8,128)}, u32[]{:S(2)}) copy-start(f32[8,12,132]{2,0,1:T(8,128)} %get-tuple-element.145) | copy-start | bytes 152068
  105.7 3.0 %copy-start.16 = (f32[8,12,132]{2,0,1:T(8,128)S(1)}, f32[8,12,132]{2,0,1:T(8,128)}, u32[]{:S(2)}) copy-start(f32[8,12,132]{2,0,1:T(8,128)} %get-tuple-element.146) | copy-start | bytes 152068
  107.8 1.0 copy-start.17
  107.8 1.0 copy-start.18
  107.8 1.0 copy-start.19
  107.8 1.0 copy-start.20
  107.8 1.1 copy-start.21
  107.8 1.1 copy-start.22
  107.8 1.1 copy-start.23
  107.8 1.2 copy-start.24
  107.8 1.2 copy-start.25
  107.9 1.2 copy-start.26
  107.9 1.2 copy-start.27
  107.9 1.2 copy-start.28
  107.9 1.3 copy-start.29
  111.4 1.0 copy-start.5
  111.4 1.0 copy-start.40
  111.4 1.0 copy-start.41
  113.9 1.0 copy-start.4
  116.3 3.0 %copy-start.35 = (pred[6,10,130]{2,0,1:T(8,128)(4,1)S(1)}, pred[6,10,130]{2,0,1:T(8,128)(4,1)}, u32[]{:S(2)}) copy-start(pred[6,10,130]{2,0,1:T(8,128)(4,1)} %slice.2547) | copy-start | bytes 23404
  220.5 0.7 copy-start.44
where the time goes:
time: 223 us; the launch traced here: 221 us
  blocking collectives  92.8 us (42%)
  starting transfers between devices  45.3 us (20%)
  other arithmetic  40.6 us (18%)
  local copies, waits for them, and re-layouts  28.8 us (13%)
  matrix products  8.62 us (4%)
  waiting for transfers between devices  2.91 us (1%)
    psum x4, blocking collectives, over_axes(): x = lax.psum(x, axis)  92.8 us
    ppermute x6, starting transfers between devices, extended(): lax.ppermute(head, axis, [((i + 1) % count, i) for i in range(count)])  37.3 us
    unnamed x72, other arithmetic  19.6 us
    ppermute x6, starting transfers between devices, extended(): lax.ppermute(tail, axis, [(i, (i + 1) % count) for i in range(count)])  8 us
    unnamed x113, local copies, waits for them, and re-layouts  7.57 us
    dot_general x36, matrix products, spread(): jnp.einsum('abc,ax,by,cz->xyz', values, table_x, table_y, table_z, precis...  7.14 us
    select_n x11, other arithmetic, substep(): link_term = jnp.where(solid_next & moving, returned + bounced, 0.0)  5.8 us
  transfers between devices with their start and end apart: 12, of which 2 were waited for; matrix products, arithmetic and copies ran while one was open for 17% of the time, Pallas kernels for 0%

commit v1 on v0

v1 whole, which is shorter than its diff:
```python
import jax
import jax.numpy as jnp
from jax import lax
from jax.experimental import pallas as pl
from jax.experimental.pallas import tpu as pltpu
from jax.sharding import Mesh
from jax.sharding import PartitionSpec as P

BOX_XY = 16
BOX_Z = 64
RADIUS = 4
GX = ("gx_0", "gx_1")

VELOCITIES = (
    (0, 0, 0),
    (1, 0, 0),
    (-1, 0, 0),
    (0, 1, 0),
    (0, -1, 0),
    (0, 0, 1),
    (0, 0, -1),
    (1, 1, 0),
    (-1, -1, 0),
    (1, -1, 0),
    (-1, 1, 0),
    (1, 0, 1),
    (-1, 0, -1),
    (1, 0, -1),
    (-1, 0, 1),
    (0, 1, 1),
    (0, -1, -1),
    (0, 1, -1),
    (0, -1, 1),
)
OPPOSITE = (0, 2, 1, 4, 3, 6, 5, 8, 7, 10, 9, 12, 11, 14, 13, 16, 15, 18, 17)
WEIGHTS = (1.0 / 3.0,) + (1.0 / 18.0,) * 6 + (1.0 / 36.0,) * 12
COARSE_RATE = 1.25
FINE_RATE = 1.0 / 1.1
HIGHEST = lax.Precision.HIGHEST
RHO = 19
BIG = 1.0e30


def heading(axis, sign):
    return tuple(q for q in range(19) if VELOCITIES[q][axis] == sign)


XP, XM = heading(0, 1), heading(0, -1)
YP, YM = heading(1, 1), heading(1, -1)
ZP, ZM = heading(2, 1), heading(2, -1)
F32 = jnp.float32
VMEM = pl.BlockSpec(memory_space=pltpu.VMEM)
SMEM = pl.BlockSpec(memory_space=pltpu.SMEM)


def along(vectors, q):
    total = None
    for d in range(3):
        sign = VELOCITIES[q][d]
        if sign == 0:
            continue
        if total is None:
            total = vectors[d] if sign == 1 else -vectors[d]
        else:
            total = total + vectors[d] if sign == 1 else total - vectors[d]
    return total


def equilibria(density, vectors):
    base = 1.0 - 1.5 * (
        vectors[0] * vectors[0] + vectors[1] * vectors[1] + vectors[2] * vectors[2]
    )
    scaled = {w: w * density for w in set(WEIGHTS)}
    out = [scaled[WEIGHTS[0]] * base]
    for q in range(1, 19, 2):
        c = along(vectors, q)
        even = base + 4.5 * c * c
        odd = 3.0 * c
        out.append(scaled[WEIGHTS[q]] * (even + odd))
        out.append(scaled[WEIGHTS[q]] * (even - odd))
    return out


def collided(p, rate):
    density = p[0]
    for q in range(1, 19):
        density = density + p[q]
    inverse = 1.0 / density
    vectors = []
    for d in range(3):
        total = None
        for q in range(19):
            sign = VELOCITIES[q][d]
            if sign == 1:
                total = p[q] if total is None else total + p[q]
        for q in range(19):
            if VELOCITIES[q][d] == -1:
                total = total - p[q]
        vectors.append(total * inverse)
    targets = equilibria(density, vectors)
    return [p[q] - rate * (p[q] - targets[q]) for q in range(19)], density


def dot(a, b):
    return lax.dot_general(
        a, b, (((1,), (0,)), ((), ())), precision=HIGHEST, preferred_element_type=F32
    )


def iota2(shape, axis):
    return lax.broadcasted_iota(jnp.int32, shape, axis)


def upsampled(tiles):
    rows = tiles.shape[0]
    r, c = iota2((rows, rows), 0), iota2((rows, rows), 1)
    left = jnp.where(((r >> 3) == (c >> 3)) & (((r & 7) >> 1) == (c & 7)), 1.0, 0.0)
    k, n = iota2((128, 128), 0), iota2((128, 128), 1)
    right = jnp.where(k == (n >> 1), 1.0, 0.0)
    return dot(left, dot(tiles, right))


def coalesced(tiles):
    rows = tiles.shape[0]
    r, c = iota2((rows, rows), 0), iota2((rows, rows), 1)
    left = jnp.where(((r >> 3) == (c >> 3)) & ((r & 7) == ((c & 7) >> 1)), 0.25, 0.0)
    k, n = iota2((128, 128), 0), iota2((128, 128), 1)
    right = jnp.where((k >> 1) == n, 1.0, 0.0)
    return dot(left, dot(tiles, right))


def collide_kernel(fine, coarse, fp, cp, xr, xl):
    gx = lax.axis_index(GX)
    last = lax.axis_size(GX) - 1
    cp[...] = jnp.zeros(cp.shape, F32)
    for x in range(4):
        post, density = collided([coarse[q, x] for q in range(19)], COARSE_RATE)
        for q in range(19):
            cp[q, x, 0:4, 0:64] = post[q]

    def plane(x, carry):
        post, density = collided([fine[q, x] for q in range(19)], FINE_RATE)
        for q in range(19):
            fp[q, x] = post[q]
        fp[RHO, x] = density
        return carry

    lax.fori_loop(0, 4, plane, 0)
    for out, near, far, inward, edge in ((xr, 3, 2, XP, last), (xl, 0, 1, XM, 0)):
        for k, q in enumerate(inward):
            out[19 + k] = fp[q, far]
        out[24] = fp[RHO, far]

        @pl.when(gx != edge)
        def _():
            out[0:19] = fp[0:19, near]
            for k, q in enumerate(inward):
                out[25 + k] = cp[q, near]

        @pl.when(gx == edge)
        def _():
            up = upsampled(cp[:, near].reshape(152, 128))
            out[0:19] = up.reshape(19, 8, 128)
            picked = jnp.concatenate([fp[q, near] for q in inward], axis=0)
            out[25:30] = coalesced(picked).reshape(5, 8, 128)


def pack_y_kernel(fp, cp, r_l, r_r, yr, yl):
    rho_l, rho_r = r_l[0], r_r[0]
    for q in range(1, 19):
        rho_l = rho_l + r_l[q]
        rho_r = rho_r + r_r[q]
    for out, near, far, cnear, inward in ((yr, 7, 6, 3, YP), (yl, 0, 1, 0, YM)):
        out[...] = jnp.zeros(out.shape, F32)
        out[0:19, 1:2] = r_l[0:19, near : near + 1]
        out[RHO, 1:2] = rho_l[near : near + 1]
        out[0:19, 6:7] = r_r[0:19, near : near + 1]
        out[RHO, 6:7] = rho_r[near : near + 1]
        for x in range(4):
            out[0:20, 2 + x : 3 + x] = fp[:, x, near : near + 1]
        for k in range(5):
            out[XP[k], 0:1] = r_l[19 + k, near : near + 1]
            out[XM[k], 7:8] = r_r[19 + k, near : near + 1]
        out[RHO, 0:1] = r_l[24, near : near + 1]
        out[RHO, 7:8] = r_r[24, near : near + 1]
        for k, q in enumerate(inward):
            out[20 + k, 1:2] = r_l[q, far : far + 1]
            out[20 + k, 6:7] = r_r[q, far : far + 1]
            for x in range(4):
                out[20 + k, 2 + x : 3 + x] = fp[q, x, far : far + 1]
                out[26 + k, 1 + x : 2 + x] = cp[q, x, cnear : cnear + 1]
            if q in XP:
                out[20 + k, 0:1] = r_l[19 + XP.index(q), far : far + 1]
                out[26 + k, 0:1] = r_l[25 + XP.index(q), cnear : cnear + 1]
            if q in XM:
                out[20 + k, 7:8] = r_r[19 + XM.index(q), far : far + 1]
                out[26 + k, 5:6] = r_r[25 + XM.index(q), cnear : cnear + 1]
        out[25, 0:1] = r_l[24, far : far + 1]
        out[25, 1:2] = rho_l[far : far + 1]
        out[25, 6:7] = rho_r[far : far + 1]
        out[25, 7:8] = r_r[24, far : far + 1]
        for x in range(4):
            out[25, 2 + x : 3 + x] = fp[RHO, x, far : far + 1]


def pack_z_kernel(fp, cp, r_l, r_r, y_l, y_r, ext, cext, zr, zl):
    for x in range(4):
        ext[:, 2 + x, 0:8] = fp[:, x]
        cext[:, 1 + x] = cp[:, x]
    cext[:, 0] = jnp.zeros((19, 8, 128), F32)
    cext[:, 5] = jnp.zeros((19, 8, 128), F32)
    for got, near, far, cplane, inward in ((r_l, 1, 0, 0, XP), (r_r, 6, 7, 5, XM)):
        ext[0:19, near, 0:8] = got[0:19]
        density = got[0]
        for q in range(1, 19):
            density = density + got[q]
        ext[RHO, near, 0:8] = density
        for k, q in enumerate(inward):
            ext[q, far, 0:8] = got[19 + k]
            cext[q, cplane] = got[25 + k]
        ext[RHO, far, 0:8] = got[24]
    for j in range(8):
        for got, near, far, crow, inward in ((y_l, 15, 14, 7, YP), (y_r, 8, 9, 4, YM)):
            ext[:, j, near : near + 1] = got[0:20, j : j + 1]
            for k, q in enumerate(inward):
                ext[q, j, far : far + 1] = got[20 + k, j : j + 1]
                if j < 6:
                    cext[q, j, crow : crow + 1] = got[26 + k, j : j + 1]
            ext[RHO, j, far : far + 1] = got[25, j : j + 1]
    lane = iota2((8, 128), 1)

    def plane(j, carry):
        for h in range(2):
            to_r = jnp.zeros((8, 128), F32)
            to_l = jnp.zeros((8, 128), F32)
            for f in range(20):
                turned = pltpu.roll(ext[f, j, 8 * h : 8 * h + 8], (2 * f + 2) % 128, 1)
                to_r = jnp.where((lane >> 1) == f, turned, to_r)
                to_l = jnp.where((lane >> 1) == f + 1, turned, to_l)
            if h == 0:
                jc = jnp.minimum(j, 5)
                for k in range(5):
                    to_r = jnp.where(lane == 64 + k, pltpu.roll(cext[ZP[k], jc], k + 1, 1), to_r)
                    to_l = jnp.where(lane == 64 + k, pltpu.roll(cext[ZM[k], jc], 64 + k, 1), to_l)
            zr[j, 8 * h : 8 * h + 8] = to_r
            zl[j, 8 * h : 8 * h + 8] = to_l
        return carry

    lax.fori_loop(0, 8, plane, 0)


def geometry_kernel(centers, velocity, code, wind):
    gx, gy, gz = lax.axis_index(GX), lax.axis_index("gy"), lax.axis_index("gz")
    row, lane = iota2((8, 128), 0), iota2((8, 128), 1)
    low_row, low_lane = row < 4, lane < 64
    nbx, nby, nbz = 4, 4, 16
    boxes = nbx * nby * nbz
    y0, z0, x0 = gy * 8, gz * 128, gx * 4
    own_y = y0 // BOX_XY
    prev_y = lax.rem(lax.div(y0 + nby * BOX_XY - 1, BOX_XY), nby)
    next_y = lax.rem(lax.div(y0 + 8, BOX_XY), nby)
    lo_z = z0 // BOX_Z
    prev_z = lax.rem(lo_z + nbz - 1, nbz)
    next_z = lax.rem(lo_z + 2, nbz)
    row_boxes = ((own_y, own_y), (next_y, prev_y))
    lane_boxes = ((lo_z, lo_z + 1), (next_z, prev_z))
    y_of = (row, jnp.where(low_row, row + 8, row - 8))
    z_of = (lane, jnp.where(low_lane, lane + 128, lane - 128))
    off_y = [((y0 + y_of[h] + BOX_XY * nby) & (BOX_XY - 1)).astype(F32) for h in range(2)]
    off_z = [((z0 + z_of[h] + BOX_Z * nbz) & (BOX_Z - 1)).astype(F32) for h in range(2)]

    def plane(j, carry):
        x = x0 + j - 2
        inside = jnp.where((x >= 0) & (x < nbx * BOX_XY), 1.0, 0.0)
        safe = jnp.clip(x, 0, nbx * BOX_XY - 1)
        bx = lax.div(safe, BOX_XY)
        off_x = lax.rem(safe, BOX_XY).astype(F32)

        def field(table, base, h, g):
            def one(by, bz):
                return table[base + (bx * nby + by) * nbz + bz].astype(F32)

            upper = jnp.where(
                low_lane,
                one(row_boxes[h][0], lane_boxes[g][0]),
                one(row_boxes[h][0], lane_boxes[g][1]),
            )
            if h == 0:
                return upper
            lower = jnp.where(
                low_lane,
                one(row_boxes[h][1], lane_boxes[g][0]),
                one(row_boxes[h][1], lane_boxes[g][1]),
            )
            return jnp.where(low_row, upper, lower)

        for h in range(2):
            for g in range(2):
                bits = jnp.zeros((8, 128), F32)
                for moment in range(3):
                    base = moment * 3 * boxes
                    gap_x = off_x - field(centers, base, h, g)
                    gap_y = off_y[h] - field(centers, base + boxes, h, g)
                    gap_z = off_z[g] - field(centers, base + 2 * boxes, h, g)
                    distance = gap_x * gap_x + gap_y * gap_y + gap_z * gap_z
                    hit = (distance <= float(RADIUS * RADIUS)) & (inside > 0.5)
                    bits = bits + jnp.where(hit, float(1 << moment), 0.0)
                code[j, h, g] = bits
                for d in range(3):
                    wind[d, j, h, g] = field(velocity, d * boxes, h, g) * inside
        return carry

    lax.fori_loop(0, 8, plane, 0)


def turned(tiles, step, axis):
    size = 8 if axis == 0 else 128
    at = iota2((8, 128), axis)
    rolled = [pltpu.roll(t, step % size, axis) for t in tiles]
    seam = at == (0 if step == 1 else size - 1)
    return [jnp.where(seam, rolled[1], rolled[0]), jnp.where(seam, rolled[0], rolled[1])]


def pull(tiles, cy, cz):
    if cz:
        tiles = [turned(tiles[h], cz, 1) for h in range(2)]
    if cy:
        first = turned([tiles[0][0], tiles[1][0]], cy, 0)
        second = turned([tiles[0][1], tiles[1][1]], cy, 0)
        tiles = [[first[0], second[0]], [first[1], second[1]]]
    return tiles


def main_kernel(ext_a, cext, z_l, z_r, code, wind, fine_next, coarse_next, force, ext_b, post, sums):
    gx, gz = lax.axis_index(GX), lax.axis_index("gz")
    last = lax.axis_size(GX) - 1
    row, lane = iota2((8, 128), 0), iota2((8, 128), 1)

    for k in range(5):
        q = ZP[k]
        for x in range(4):
            j = 1 + x - VELOCITIES[q][0]
            tile = jnp.where(lane == 127, pltpu.roll(z_l[j, 0:8], 63 - k, 1), cext[q, j])
            tile = pltpu.roll(tile, 1, 1)
            if VELOCITIES[q][1]:
                tile = pltpu.roll(tile, VELOCITIES[q][1] % 8, 0)
            coarse_next[q, x] = tile[0:4, 0:64]
        q = ZM[k]
        for x in range(4):
            j = 1 + x - VELOCITIES[q][0]
            tile = z_r[j, 0:8]
            if k:
                tile = pltpu.roll(tile, 128 - k, 1)
            tile = jnp.where(lane == 64, tile, cext[q, j])
            tile = pltpu.roll(tile, 127, 1)
            if VELOCITIES[q][1]:
                tile = pltpu.roll(tile, VELOCITIES[q][1] % 8, 0)
            coarse_next[q, x] = tile[0:4, 0:64]
    for q in range(19):
        if VELOCITIES[q][2] == 0:
            for x in range(4):
                tile = cext[q, 1 + x - VELOCITIES[q][0]]
                if VELOCITIES[q][1]:
                    tile = pltpu.roll(tile, VELOCITIES[q][1] % 8, 0)
                coarse_next[q, x] = tile[0:4, 0:64]

    def unpack(j, carry):
        for h in range(2):
            from_l = z_l[j, 8 * h : 8 * h + 8]
            from_r = z_r[j, 8 * h : 8 * h + 8]
            for f in range(20):
                before = pltpu.roll(from_l, (126 - 2 * f) % 128, 1)
                after = pltpu.roll(from_r, (126 - 2 * f) % 128, 1)
                ext_b[f, j, 8 * h : 8 * h + 8] = jnp.where(lane < 64, after, before)
        return carry

    lax.fori_loop(0, 8, unpack, 0)

    def substep(get, prev_bit, new_bit, first, stop, store, halves):
        def bits(j, h, g):
            return code[j, h, g].astype(jnp.int32)

        def prepare(j, carry):
            rho_open, open_ = [[None] * 2, [None] * 2], [[None] * 2, [None] * 2]
            for h in range(2):
                for g in range(2):
                    is_open = (bits(j, h, g) & (prev_bit | new_bit)) == 0
                    open_[h][g] = jnp.where(is_open, 1.0, 0.0)
                    rho_open[h][g] = jnp.where(is_open, get(RHO, j, h, g), 0.0)
            for n, tiles in enumerate((rho_open, open_)):
                back, forth = pull(tiles, 0, 1), pull(tiles, 0, -1)
                side_z = [[back[h][g] + forth[h][g] for g in range(2)] for h in range(2)]
                down, up = pull(tiles, 1, 0), pull(tiles, -1, 0)
                down2, up2 = pull(side_z, 1, 0), pull(side_z, -1, 0)
                for h in halves:
                    for g in halves:
                        side_y = down[h][g] + up[h][g]
                        both = down2[h][g] + up2[h][g]
                        sums[2 * n, j, h, g] = 2.0 * (side_y + side_z[h][g]) + both
                        sums[2 * n + 1, j, h, g] = 2.0 * tiles[h][g] + side_y + side_z[h][g]
            return carry

        lax.fori_loop(first - 1, stop + 1, prepare, 0)

        def plane(j, carry):
            pushes = list(carry)
            mine = [[bits(j, h, g) for g in range(2)] for h in range(2)]
            rho = [[get(RHO, j, h, g) for g in range(2)] for h in range(2)]
            covered, uncovered, refill = {}, {}, {}
            for h in halves:
                for g in halves:
                    covered[h, g] = (mine[h][g] & new_bit) != 0
                    uncovered[h, g] = (mine[h][g] & prev_bit) != 0
                    above = (
                        12.0 * rho[h][g]
                        + sums[0, j, h, g]
                        + (sums[1, j - 1, h, g] + sums[1, j + 1, h, g])
                    )
                    below = 12.0 + sums[2, j, h, g] + (sums[3, j - 1, h, g] + sums[3, j + 1, h, g])
                    density = above / below
                    own = [wind[d, j, h, g] for d in range(3)]
                    refill[h, g] = equilibria(density, own)
            own = [wind[d, j, 0, 0] for d in range(3)]
            for q in range(19):
                cx, cy, cz = VELOCITIES[q]
                weight = 6.0 * WEIGHTS[q]
                if q == 0:
                    for h in halves:
                        for g in halves:
                            p0 = get(0, j, h, g)
                            kept = jnp.where(uncovered[h, g], refill[h, g][0], p0)
                            store(0, j, h, g, jnp.where(covered[h, g], p0, kept))
                    continue
                src = j - cx
                ghost = jnp.logical_or(
                    jnp.logical_and(gx == 0, src < 2), jnp.logical_and(gx == last, src > 5)
                )
                fluid = jnp.where(ghost, 2.0 * BIG, BIG)
                state = [[None] * 2, [None] * 2]
                for h in range(2):
                    for g in range(2):
                        b = bits(src, h, g)
                        push = weight * along([wind[d, src, h, g] for d in range(3)], q)
                        state[h][g] = jnp.where(
                            (b & new_bit) != 0,
                            push,
                            jnp.where((b & prev_bit) != 0, 2.0 * BIG, fluid),
                        )
                state = pull(state, cy, cz)
                came = pull(
                    [[get(q, src, h, g) for g in range(2)] for h in range(2)], cy, cz
                )
                for h in halves:
                    for g in halves:
                        bounced = (
                            get(OPPOSITE[q], j, h, g) + state[h][g] * rho[h][g]
                        )
                        arrived = jnp.where(state[h][g] < 0.5 * BIG, bounced, came[h][g])
                        kept = jnp.where(uncovered[h, g], refill[h, g][q], arrived)
                        store(q, j, h, g, jnp.where(covered[h, g], get(q, j, h, g), kept))
                dens = pull([[get(RHO, src, h, g) for g in range(2)] for h in range(2)], cy, cz)
                term = 2.0 * came[0][0] - (weight * along(own, q)) * dens[0][0]
                linked = (state[0][0] > 0.5 * BIG) & (state[0][0] < 1.5 * BIG) & covered[0, 0]
                term = jnp.where(linked, term, 0.0)
                for d in range(3):
                    if VELOCITIES[q][d] == 1:
                        pushes[d] = pushes[d] + term
                    elif VELOCITIES[q][d] == -1:
                        pushes[d] = pushes[d] - term
            keep = jnp.logical_and(j >= 2, j <= 5)
            return tuple(jnp.where(keep, new, old) for new, old in zip(pushes, carry))

        zero = jnp.zeros((8, 128), F32)
        return lax.fori_loop(first, stop, plane, (zero, zero, zero))

    def get_first(f, j, h, g):
        return (ext_a, ext_b)[g][f, j, 8 * h : 8 * h + 8]

    def get_second(f, j, h, g):
        return post[f, j, h, g]

    def store_first(q, j, h, g, value):
        post[q, j, h, g] = value

    def store_second(q, j, h, g, value):
        fine_next[q, j - 2] = value

    first = substep(get_first, 1, 2, 1, 7, store_first, (0, 1))

    def relax(n, carry):
        j, h, g = 1 + n // 4, (n // 2) % 2, n % 2
        out, density = collided([post[q, j, h, g] for q in range(19)], FINE_RATE)
        for q in range(19):
            post[q, j, h, g] = out[q]
        post[RHO, j, h, g] = density
        return carry

    lax.fori_loop(0, 24, relax, 0)
    for edge, j in ((0, 1), (last, 6)):

        @pl.when(gx == edge)
        def _():
            for h in range(2):
                for g in range(2):
                    for f in range(20):
                        post[f, j, h, g] = get_first(f, j, h, g)

    second = substep(get_second, 2, 4, 2, 6, store_second, (0,))
    line = iota2((1, 128), 1)
    total = jnp.zeros((1, 128), F32)
    for n, value in enumerate(first + second):
        columns = jnp.sum(value, axis=0, keepdims=True)
        low = jnp.sum(jnp.where(line < 64, columns, 0.0), axis=1, keepdims=True)
        high = jnp.sum(jnp.where(line >= 64, columns, 0.0), axis=1, keepdims=True)
        at = n * 16 + 2 * gz
        total = jnp.where(line == at, low, jnp.where(line == at + 1, high, total))
    force[...] = jnp.broadcast_to(total, (8, 128))


def spread_kernel(got, out):
    out[...] = jnp.broadcast_to(jnp.sum(got[...], axis=0, keepdims=True), out.shape)


def boxes_kernel(got, out):
    b, r = iota2((16, 128), 0), iota2((16, 128), 1)
    pick = jnp.where(((b >> 2) == (r >> 5)) & ((b & 3) == ((r & 7) >> 1)), 1.0, 0.0)
    table = dot(pick, got[...])
    for n in range(6):
        rolled = pltpu.roll(table, (128 - 16 * n) % 128, 1) if n else table
        for bx in range(4):
            out[n // 3, n % 3, bx] = rolled[4 * bx : 4 * bx + 4, 0:16]


def call(kernel, shapes, operands, specs=None, scratch=(), name=None):
    return pl.pallas_call(
        kernel,
        out_shape=[jax.ShapeDtypeStruct(s, F32) for s in shapes],
        in_specs=specs or [VMEM] * len(operands),
        out_specs=[VMEM] * len(shapes),
        scratch_shapes=list(scratch),
        name=name,
    )(*operands)


def swapped(up, down, axis):
    count = lax.axis_size(axis)
    from_low = lax.ppermute(up, axis, [(i, (i + 1) % count) for i in range(count)])
    from_high = lax.ppermute(down, axis, [((i + 1) % count, i) for i in range(count)])
    return from_low, from_high


def shards(coarse_pdfs, fine_pdfs, centers, sphere_velocity):
    fp, cp, xr, xl = call(
        collide_kernel,
        ((20, 4, 8, 128), (19, 4, 8, 128), (30, 8, 128), (30, 8, 128)),
        (fine_pdfs, coarse_pdfs),
        name="collide",
    )
    code, wind = call(
        geometry_kernel,
        ((8, 2, 2, 8, 128), (3, 8, 2, 2, 8, 128)),
        (centers.reshape(-1), sphere_velocity.reshape(-1)),
        specs=[SMEM, SMEM],
        name="geometry",
    )
    r_l, r_r = swapped(xr, xl, GX)
    yr, yl = call(
        pack_y_kernel, ((31, 8, 128), (31, 8, 128)), (fp, cp, r_l, r_r), name="pack_y"
    )
    y_l, y_r = swapped(yr, yl, "gy")
    ext, cext, zr, zl = call(
        pack_z_kernel,
        ((20, 8, 16, 128), (19, 6, 8, 128), (8, 16, 128), (8, 16, 128)),
        (fp, cp, r_l, r_r, y_l, y_r),
        name="pack_z",
    )
    z_l, z_r = swapped(zr, zl, "gz")
    fine_next, coarse_next, force = call(
        main_kernel,
        (fine_pdfs.shape, coarse_pdfs.shape, (8, 128)),
        (ext, cext, z_l, z_r, code, wind),
        scratch=(
            pltpu.VMEM((20, 8, 16, 128), F32),
            pltpu.VMEM((20, 8, 2, 2, 8, 128), F32),
            pltpu.VMEM((4, 8, 2, 2, 8, 128), F32),
        ),
        name="main",
    )
    column = lax.all_to_all(force, "gz", 0, 0, tiled=True)
    (rows,) = call(spread_kernel, ((128, 128),), (column,), name="spread")
    rows = lax.all_to_all(rows, ("gx_0", "gx_1", "gy"), 0, 0, tiled=True)
    (sphere_force,) = call(boxes_kernel, ((2, 3, 4, 4, 16),), (rows,), name="boxes")
    return coarse_next, fine_next, sphere_force


def solution(mesh):
    split = Mesh(
        mesh.devices.reshape(8, 2, mesh.shape["gy"], mesh.shape["gz"]), ("gx_0", "gx_1", "gy", "gz")
    )
    return jax.shard_map(
        shards,
        mesh=split,
        in_specs=(P(None, GX, "gy", "gz"), P(None, GX, "gy", "gz"), P(), P()),
        out_specs=(P(None, GX, "gy", "gz"), P(None, GX, "gy", "gz"), P()),
        check_vma=False,
    )
```

time: 223 us -> 102 us (0.46)
  the two profiles are of different devices: /device:TPU:16 before, /device:TPU:1 now
where the time goes in v1:
time: 102 us; the launch traced here: 101 us
  blocking collectives  37.7 us (37%)
  starting transfers between devices  33 us (32%)
  Pallas kernels  23 us (23%)
  waiting for transfers between devices  3.39 us (3%)
  local copies, waits for them, and re-layouts  3.32 us (3%)
    all_to_all x1, blocking collectives, shards(): rows = lax.all_to_all(rows, ('gx_0', 'gx_1', 'gy'), 0, 0, tiled=True)  27.5 us
    ppermute x3, starting transfers between devices, swapped(): lax.ppermute(down, axis, [((i + 1) % count, i) for i in range(count)])  26.6 us
    pallas_call x7, Pallas kernels, call(): pl.pallas_call(kernel, out_shape=[jax.ShapeDtypeStruct(s, F32) for s in s...  23 us
    all_to_all x1, blocking collectives, shards(): column = lax.all_to_all(force, 'gz', 0, 0, tiled=True)  10.2 us
    ppermute x3, starting transfers between devices, swapped(): lax.ppermute(up, axis, [(i, (i + 1) % count) for i in range(count)])  6.41 us
  transfers between devices with their start and end apart: 6, of which 4 were waited for; matrix products, arithmetic and copies ran while one was open for 1% of the time, Pallas kernels for 3%

profile of v1, /device:TPU:1, one launch (start us, length us, event | category | flops | bytes accessed | tf_op | source)
XLA Modules:
  0.0 101.1 jit_solution(18402286654383965342)
XLA Ops:
  0.6 0.0 copy-start.4
  0.6 0.0 copy-start.7
  0.7 2.3 %collide.1 = (f32[20,4,8,128]{3,2,1,0:T(8,128)}, f32[19,4,8,128]{3,2,1,0:T(8,128)}, f32[30,8,128]{2,1,0:T(8,128)}, f32[30,8,128]{2,1,0:T(8,128)}) custom-call(f32[19,4,8,128]{3,2,1,0:T(8,128)} %fine.1, f32[19,4,4,64]{3,2,1,0:T(4,128)} %coarse.1), custom_call_target="tpu_custom_call" | custom-call | tf_op jit(solution)/shard_map/collide/pallas_call | solution.py:535
  3.0 2.6 %collective-permute-start = (f32[30,8,128]{2,1,0:T(8,128)}, f32[30,8,128]{2,1,0:T(8,128)S(1)}, u32[]{:S(2)}, u32[]{:S(2)}) collective-permute-start(f32[30,8,128]{2,1,0:T(8,128)} %get-tuple-element.20), channel_id=1, source_target_pairs={{0,64},{64,128},{128,192},{192,256},{256,320},{320,384},{384,448},... | collective-permute-start | bytes 368648 | tf_op jit(solution)/shard_map/ppermute | solution.py:547
  5.6 12.4 %collective-permute-start.1 = (f32[30,8,128]{2,1,0:T(8,128)}, f32[30,8,128]{2,1,0:T(8,128)S(1)}, u32[]{:S(2)}, u32[]{:S(2)}) collective-permute-start(f32[30,8,128]{2,1,0:T(8,128)} %get-tuple-element.21), channel_id=1, source_target_pairs={{64,0},{128,64},{192,128},{256,192},{320,256},{384,320},{448,384},... | collective-permute-start | bytes 368648 | tf_op jit(solution)/shard_map/ppermute | solution.py:548
  18.0 1.0 %collective-permute-done.r_l = f32[30,8,128]{2,1,0:T(8,128)S(1)} collective-permute-done((f32[30,8,128]{2,1,0:T(8,128)}, f32[30,8,128]{2,1,0:T(8,128)S(1)}, u32[]{:S(2)}, u32[]{:S(2)}) %collective-permute-start) | collective-permute-done | bytes 122912 | tf_op jit(solution)/shard_map/ppermute | solution.py:547
  19.0 0.0 copy-start
  19.0 0.1 collective-permute-done.1.r_r
  19.2 0.0 copy-start.1
  19.2 0.5 copy-done
  19.7 0.1 copy-done.1
  19.8 2.0 %pack_y.1 = (f32[31,8,128]{2,1,0:T(8,128)}, f32[31,8,128]{2,1,0:T(8,128)}) custom-call(f32[20,4,8,128]{3,2,1,0:T(8,128)} %get-tuple-element.18.fp, f32[19,4,8,128]{3,2,1,0:T(8,128)} %get-tuple-element.19.cp, f32[30,8,128]{2,1,0:T(8,128)} %copy-done, f32[30,8,128]{2,1,0:T(8,128)} %copy-done.1), custom_call_target="tpu_custom_call" | custom-call | tf_op jit(solution)/shard_map/pack_y/pallas_call | solution.py:535
  21.8 1.9 %collective-permute-start.2 = (f32[31,8,128]{2,1,0:T(8,128)}, f32[31,8,128]{2,1,0:T(8,128)S(1)}, u32[]{:S(2)}, u32[]{:S(2)}) collective-permute-start(f32[31,8,128]{2,1,0:T(8,128)} %get-tuple-element.22), channel_id=1, source_target_pairs={{0,8},{8,16},{16,24},{24,32},{32,40},{40,48},{48,56},{56,0},{1,9},... | collective-permute-start | bytes 380936 | tf_op jit(solution)/shard_map/ppermute | solution.py:547
  23.7 4.6 %collective-permute-start.3 = (f32[31,8,128]{2,1,0:T(8,128)}, f32[31,8,128]{2,1,0:T(8,128)S(1)}, u32[]{:S(2)}, u32[]{:S(2)}) collective-permute-start(f32[31,8,128]{2,1,0:T(8,128)} %get-tuple-element.23), channel_id=1, source_target_pairs={{8,0},{16,8},{24,16},{32,24},{40,32},{48,40},{56,48},{0,56},{9,1},... | collective-permute-start | bytes 380936 | tf_op jit(solution)/shard_map/ppermute | solution.py:548
  28.3 0.6 collective-permute-done.2.y_l
  28.9 0.0 copy-start.2
  28.9 1.6 %collective-permute-done.3.y_r = f32[31,8,128]{2,1,0:T(8,128)S(1)} collective-permute-done((f32[31,8,128]{2,1,0:T(8,128)}, f32[31,8,128]{2,1,0:T(8,128)S(1)}, u32[]{:S(2)}, u32[]{:S(2)}) %collective-permute-start.3) | collective-permute-done | bytes 127008 | tf_op jit(solution)/shard_map/ppermute | solution.py:548
  30.5 0.0 copy-done.2
  30.5 0.0 copy-start.3
  30.5 0.7 copy-done.3
  31.2 3.7 %pack_z.1 = (f32[20,8,16,128]{3,2,1,0:T(8,128)}, f32[19,6,8,128]{3,2,1,0:T(8,128)}, f32[8,16,128]{2,1,0:T(8,128)}, f32[8,16,128]{2,1,0:T(8,128)}) custom-call(f32[20,4,8,128]{3,2,1,0:T(8,128)} %get-tuple-element.18.fp, f32[19,4,8,128]{3,2,1,0:T(8,128)} %get-tuple-element.19.cp, f32[30,8,128]{2,1,0:T(8,128)} %copy-done, f32[30,8,128]{2,1,0:T(8,128)} %copy-done.1, ...), custom_call_target="tpu_custom_call" | custom-call | tf_op jit(solution)/shard_map/pack_z/pallas_call | solution.py:535
  34.9 1.9 %collective-permute-start.4 = (f32[8,16,128]{2,1,0:T(8,128)}, f32[8,16,128]{2,1,0:T(8,128)S(1)}, u32[]{:S(2)}, u32[]{:S(2)}) collective-permute-start(f32[8,16,128]{2,1,0:T(8,128)} %get-tuple-element.26), channel_id=1, source_target_pairs={{0,1},{1,2},{2,3},{3,4},{4,5},{5,6},{6,7},{7,0},{8,9},{9,10},{10,1... | collective-permute-start | bytes 196616 | tf_op jit(solution)/shard_map/ppermute | solution.py:547
  36.8 9.6 %collective-permute-start.5 = (f32[8,16,128]{2,1,0:T(8,128)}, f32[8,16,128]{2,1,0:T(8,128)S(1)}, u32[]{:S(2)}, u32[]{:S(2)}) collective-permute-start(f32[8,16,128]{2,1,0:T(8,128)} %get-tuple-element.27), channel_id=1, source_target_pairs={{1,0},{2,1},{3,2},{4,3},{5,4},{6,5},{7,6},{0,7},{9,8},{10,9},{11,1... | collective-permute-start | bytes 196616 | tf_op jit(solution)/shard_map/ppermute | solution.py:548
  46.5 0.0 copy-done.4
  46.5 0.7 reshape.16.centers
  47.2 0.0 copy-done.7
  47.2 0.7 reshape.17.velocity
  47.9 3.0 %geometry.1 = (f32[8,2,2,8,128]{4,3,2,1,0:T(8,128)}, f32[3,8,2,2,8,128]{5,4,3,2,1,0:T(8,128)}) custom-call(s32[2304]{0:T(1024)} %reshape.16.centers, f32[768]{0:T(1024)} %reshape.17.velocity), custom_call_target="tpu_custom_call" | custom-call | tf_op jit(solution)/shard_map/geometry/pallas_call | solution.py:535
  50.9 0.0 collective-permute-done.4.z_l
  50.9 0.0 copy-start.5
  50.9 0.0 collective-permute-done.5.z_r
  50.9 0.0 copy-start.6
  50.9 0.6 copy-done.5
  51.5 0.0 copy-done.6
  51.5 8.9 %main.1 = (f32[19,4,8,128]{3,2,1,0:T(8,128)}, f32[19,4,4,64]{3,2,1,0:T(4,128)}, f32[8,128]{1,0:T(8,128)}) custom-call(f32[20,8,16,128]{3,2,1,0:T(8,128)} %get-tuple-element.24.ext_a, f32[19,6,8,128]{3,2,1,0:T(8,128)} %get-tuple-element.25.cext, f32[8,16,128]{2,1,0:T(8,128)} %copy-done.5, f32[8,16,128]{2,1,0:T(8,128)} %copy-done.6, ...), custom_call_target="tpu_custom_call" | custom-call | tf_op jit(solution)/shard_map/main/pallas_call | solution.py:535
  60.4 10.2 %all_to_all.22 = f32[8,1,128]{2,1,0:T(1,128)} all-to-all(f32[8,1,128]{2,1,0:T(1,128)} %bitcast.11), channel_id=1, replica_groups=mesh['gx_0'=8,'gx_1'=2,'gy'=8,'gz'=8] {'gz'}, dimensions={0} | all-to-all | bytes 8192 | tf_op jit(solution)/shard_map/all_to_all | solution.py:589
  70.6 1.3 %spread.1 = f32[128,128]{1,0:T(8,128)} custom-call(f32[8,128]{1,0:T(8,128)} %bitcast.10), custom_call_target="tpu_custom_call" | custom-call | tf_op jit(solution)/shard_map/spread/pallas_call | solution.py:535
  71.9 27.5 %all_to_all.23 = f32[128,1,128]{2,1,0:T(1,128)} all-to-all(f32[128,1,128]{2,1,0:T(1,128)} %bitcast.9), channel_id=1, replica_groups=mesh['gx_0'=8,'gx_1'=2,'gy'=8,'gz'=8] {'gx_0','gx_1','gy'}, dimensions={0} | all-to-all | bytes 131072 | tf_op jit(solution)/shard_map/all_to_all | solution.py:591
  99.4 1.7 %boxes.1 = f32[2,3,4,4,16]{4,3,2,1,0:T(4,128)} custom-call(f32[128,128]{1,0:T(8,128)} %bitcast.8), custom_call_target="tpu_custom_call" | custom-call | tf_op jit(solution)/shard_map/boxes/pallas_call | solution.py:535
Async XLA Ops:
  0.6 45.8 %copy-start.4 = (s32[3,3,4,4,16]{4,3,2,1,0:T(4,128)S(1)}, s32[3,3,4,4,16]{4,3,2,1,0:T(4,128)}, u32[]{:S(2)}) copy-start(s32[3,3,4,4,16]{4,3,2,1,0:T(4,128)} %param.6) | copy-start | bytes 27652
  0.6 46.5 %copy-start.7 = (f32[3,4,4,16]{3,2,1,0:T(4,128)S(1)}, f32[3,4,4,16]{3,2,1,0:T(4,128)}, u32[]{:S(2)}) copy-start(f32[3,4,4,16]{3,2,1,0:T(4,128)} %param.7) | copy-start | bytes 9220
  3.0 16.1 %collective-permute-start = (f32[30,8,128]{2,1,0:T(8,128)}, f32[30,8,128]{2,1,0:T(8,128)S(1)}, u32[]{:S(2)}, u32[]{:S(2)}) collective-permute-start(f32[30,8,128]{2,1,0:T(8,128)} %get-tuple-element.20), channel_id=1, source_target_pairs={{0,64},{64,128},{128,192},{192,256},{256,320},{320,384},{384,448},... | collective-permute-start | bytes 368648 | tf_op jit(solution)/shard_map/ppermute | solution.py:547
  5.6 13.6 %collective-permute-start.1 = (f32[30,8,128]{2,1,0:T(8,128)}, f32[30,8,128]{2,1,0:T(8,128)S(1)}, u32[]{:S(2)}, u32[]{:S(2)}) collective-permute-start(f32[30,8,128]{2,1,0:T(8,128)} %get-tuple-element.21), channel_id=1, source_target_pairs={{64,0},{128,64},{192,128},{256,192},{320,256},{384,320},{448,384},... | collective-permute-start | bytes 368648 | tf_op jit(solution)/shard_map/ppermute | solution.py:548
  19.0 0.6 copy-start
  19.2 0.6 copy-start.1
  21.8 7.1 %collective-permute-start.2 = (f32[31,8,128]{2,1,0:T(8,128)}, f32[31,8,128]{2,1,0:T(8,128)S(1)}, u32[]{:S(2)}, u32[]{:S(2)}) collective-permute-start(f32[31,8,128]{2,1,0:T(8,128)} %get-tuple-element.22), channel_id=1, source_target_pairs={{0,8},{8,16},{16,24},{24,32},{32,40},{40,48},{48,56},{56,0},{1,9},... | collective-permute-start | bytes 380936 | tf_op jit(solution)/shard_map/ppermute | solution.py:547
  23.7 6.8 %collective-permute-start.3 = (f32[31,8,128]{2,1,0:T(8,128)}, f32[31,8,128]{2,1,0:T(8,128)S(1)}, u32[]{:S(2)}, u32[]{:S(2)}) collective-permute-start(f32[31,8,128]{2,1,0:T(8,128)} %get-tuple-element.23), channel_id=1, source_target_pairs={{8,0},{16,8},{24,16},{32,24},{40,32},{48,40},{56,48},{0,56},{9,1},... | collective-permute-start | bytes 380936 | tf_op jit(solution)/shard_map/ppermute | solution.py:548
  28.9 1.6 %copy-start.2 = (f32[31,8,128]{2,1,0:T(8,128)}, f32[31,8,128]{2,1,0:T(8,128)S(1)}, u32[]{:S(2)}) copy-start(f32[31,8,128]{2,1,0:T(8,128)S(1)} %collective-permute-done.2.y_l) | copy-start | bytes 380932
  30.5 0.7 copy-start.3
  34.9 16.0 %collective-permute-start.4 = (f32[8,16,128]{2,1,0:T(8,128)}, f32[8,16,128]{2,1,0:T(8,128)S(1)}, u32[]{:S(2)}, u32[]{:S(2)}) collective-permute-start(f32[8,16,128]{2,1,0:T(8,128)} %get-tuple-element.26), channel_id=1, source_target_pairs={{0,1},{1,2},{2,3},{3,4},{4,5},{5,6},{6,7},{7,0},{8,9},{9,10},{10,1... | collective-permute-start | bytes 196616 | tf_op jit(solution)/shard_map/ppermute | solution.py:547
  36.8 14.1 %collective-permute-start.5 = (f32[8,16,128]{2,1,0:T(8,128)}, f32[8,16,128]{2,1,0:T(8,128)S(1)}, u32[]{:S(2)}, u32[]{:S(2)}) collective-permute-start(f32[8,16,128]{2,1,0:T(8,128)} %get-tuple-element.27), channel_id=1, source_target_pairs={{1,0},{2,1},{3,2},{4,3},{5,4},{6,5},{7,6},{0,7},{9,8},{10,9},{11,1... | collective-permute-start | bytes 196616 | tf_op jit(solution)/shard_map/ppermute | solution.py:548
  50.9 0.6 copy-start.5
  50.9 0.6 copy-start.6

commit v2 on v1

--- a/solution.py
+++ b/solution.py
@@ -10,6 +10,7 @@
 BOX_Z = 64
 RADIUS = 4
 GX = ("gx_0", "gx_1")
+GY = ("gy_0", "gy_1")
 
 VELOCITIES = (
     (0, 0, 0),
@@ -51,6 +52,7 @@
 F32 = jnp.float32
 VMEM = pl.BlockSpec(memory_space=pltpu.VMEM)
 SMEM = pl.BlockSpec(memory_space=pltpu.SMEM)
+ANY = pl.BlockSpec(memory_space=pl.ANY)
 
 
 def along(vectors, q):
@@ -165,7 +167,7 @@
             out[25:30] = coalesced(picked).reshape(5, 8, 128)
 
 
-def pack_y_kernel(fp, cp, r_l, r_r, yr, yl):
+def pack_y_kernel(fp, cp, r_l, r_r, after, yr, yl):
     rho_l, rho_r = r_l[0], r_r[0]
     for q in range(1, 19):
         rho_l = rho_l + r_l[q]
@@ -249,8 +251,8 @@
     lax.fori_loop(0, 8, plane, 0)
 
 
-def geometry_kernel(centers, velocity, code, wind):
-    gx, gy, gz = lax.axis_index(GX), lax.axis_index("gy"), lax.axis_index("gz")
+def geometry_kernel(centers, velocity, after, code, wind):
+    gx, gy, gz = lax.axis_index(GX), lax.axis_index(GY), lax.axis_index("gz")
     row, lane = iota2((8, 128), 0), iota2((8, 128), 1)
     low_row, low_lane = row < 4, lane < 64
     nbx, nby, nbz = 4, 4, 16
@@ -514,7 +516,7 @@
         high = jnp.sum(jnp.where(line >= 64, columns, 0.0), axis=1, keepdims=True)
         at = n * 16 + 2 * gz
         total = jnp.where(line == at, low, jnp.where(line == at + 1, high, total))
-    force[...] = jnp.broadcast_to(total, (8, 128))
+    force[...] = jnp.broadcast_to(total, (32, 128))
 
 
 def spread_kernel(got, out):
@@ -522,8 +524,8 @@
 
 
 def boxes_kernel(got, out):
-    b, r = iota2((16, 128), 0), iota2((16, 128), 1)
-    pick = jnp.where(((b >> 2) == (r >> 5)) & ((b & 3) == ((r & 7) >> 1)), 1.0, 0.0)
+    b, r = iota2((16, 32), 0), iota2((16, 32), 1)
+    pick = jnp.where(((b >> 2) == (r >> 3)) & ((b & 3) == (r & 3)), 1.0, 0.0)
     table = dot(pick, got[...])
     for n in range(6):
         rolled = pltpu.roll(table, (128 - 16 * n) % 128, 1) if n else table
@@ -531,13 +533,19 @@
             out[n // 3, n % 3, bx] = rolled[4 * bx : 4 * bx + 4, 0:16]
 
 
-def call(kernel, shapes, operands, specs=None, scratch=(), name=None):
+def call(kernel, shapes, operands, specs=None, scratch=(), name=None, keep=True, near=None):
+    near = [s is not SMEM for s in specs or [VMEM] * len(operands)] if near is None else near
+    operands = [
+        pltpu.with_memory_space_constraint(x, pltpu.VMEM) if n else x
+        for x, n in zip(operands, near)
+    ]
     return pl.pallas_call(
         kernel,
-        out_shape=[jax.ShapeDtypeStruct(s, F32) for s in shapes],
+        out_shape=[(pltpu.VMEM if keep else jax.ShapeDtypeStruct)(s, F32) for s in shapes],
         in_specs=specs or [VMEM] * len(operands),
         out_specs=[VMEM] * len(shapes),
         scratch_shapes=list(scratch),
+        compiler_params=pltpu.CompilerParams(vmem_limit_bytes=24 * 2**20),
         name=name,
     )(*operands)
 
@@ -554,20 +562,25 @@
         collide_kernel,
         ((20, 4, 8, 128), (19, 4, 8, 128), (30, 8, 128), (30, 8, 128)),
         (fine_pdfs, coarse_pdfs),
+        near=[False] * 2,
         name="collide",
     )
     code, wind = call(
         geometry_kernel,
         ((8, 2, 2, 8, 128), (3, 8, 2, 2, 8, 128)),
-        (centers.reshape(-1), sphere_velocity.reshape(-1)),
-        specs=[SMEM, SMEM],
+        (centers.reshape(-1), sphere_velocity.reshape(-1), xr),
+        specs=[SMEM, SMEM, ANY],
         name="geometry",
     )
     r_l, r_r = swapped(xr, xl, GX)
     yr, yl = call(
-        pack_y_kernel, ((31, 8, 128), (31, 8, 128)), (fp, cp, r_l, r_r), name="pack_y"
-    )
-    y_l, y_r = swapped(yr, yl, "gy")
+        pack_y_kernel,
+        ((31, 8, 128), (31, 8, 128)),
+        (fp, cp, r_l, r_r, code),
+        specs=[VMEM] * 4 + [ANY],
+        name="pack_y",
+    )
+    y_l, y_r = swapped(yr, yl, GY)
     ext, cext, zr, zl = call(
         pack_z_kernel,
         ((20, 8, 16, 128), (19, 6, 8, 128), (8, 16, 128), (8, 16, 128)),
@@ -577,8 +590,9 @@
     z_l, z_r = swapped(zr, zl, "gz")
     fine_next, coarse_next, force = call(
         main_kernel,
-        (fine_pdfs.shape, coarse_pdfs.shape, (8, 128)),
+        (fine_pdfs.shape, coarse_pdfs.shape, (32, 128)),
         (ext, cext, z_l, z_r, code, wind),
+        keep=False,
         scratch=(
             pltpu.VMEM((20, 8, 16, 128), F32),
             pltpu.VMEM((20, 8, 2, 2, 8, 128), F32),
@@ -586,21 +600,21 @@
         ),
         name="main",
     )
-    column = lax.all_to_all(force, "gz", 0, 0, tiled=True)
-    (rows,) = call(spread_kernel, ((128, 128),), (column,), name="spread")
-    rows = lax.all_to_all(rows, ("gx_0", "gx_1", "gy"), 0, 0, tiled=True)
-    (sphere_force,) = call(boxes_kernel, ((2, 3, 4, 4, 16),), (rows,), name="boxes")
+    column = lax.all_to_all(force, ("gx_1", "gy_1", "gz"), 0, 0, tiled=True)
+    (rows,) = call(spread_kernel, ((32, 128),), (column,), near=[False], name="spread", keep=False)
+    rows = lax.all_to_all(rows, ("gx_0", "gy_0"), 0, 0, tiled=True)
+    (sphere_force,) = call(boxes_kernel, ((2, 3, 4, 4, 16),), (rows,), near=[False], name="boxes", keep=False)
     return coarse_next, fine_next, sphere_force
 
 
 def solution(mesh):
     split = Mesh(
-        mesh.devices.reshape(8, 2, mesh.shape["gy"], mesh.shape["gz"]), ("gx_0", "gx_1", "gy", "gz")
+        mesh.devices.reshape(8, 2, 4, 2, mesh.shape["gz"]), ("gx_0", "gx_1", "gy_0", "gy_1", "gz")
     )
     return jax.shard_map(
         shards,
         mesh=split,
-        in_specs=(P(None, GX, "gy", "gz"), P(None, GX, "gy", "gz"), P(), P()),
-        out_specs=(P(None, GX, "gy", "gz"), P(None, GX, "gy", "gz"), P()),
+        in_specs=(P(None, GX, GY, "gz"), P(None, GX, GY, "gz"), P(), P()),
+        out_specs=(P(None, GX, GY, "gz"), P(None, GX, GY, "gz"), P()),
         check_vma=False,
     )

time: 102 us -> 87.9 us (0.86)
  Pallas kernels: 23 us -> 12 us
  starting transfers between devices: 33 us -> 29.4 us
    pallas_call x7, Pallas kernels: 23 us -> 12 us  [call(): pl.pallas_call(kernel, out_shape=[(pltpu.VMEM if keep else jax.ShapeDtype...]
    ppermute x3, starting transfers between devices: 6.41 us -> 3.84 us  [swapped(): lax.ppermute(up, axis, [(i, (i + 1) % count) for i in range(count)])]
    ppermute x3, waiting for transfers between devices: 1.62 us -> 0.38 us  [swapped(): lax.ppermute(up, axis, [(i, (i + 1) % count) for i in range(count)])]
    ppermute x3, starting transfers between devices: 26.6 us -> 25.5 us  [swapped(): lax.ppermute(down, axis, [((i + 1) % count, i) for i in range(count)])]
    ppermute x3, waiting for transfers between devices: 1.77 us -> 2.82 us  [swapped(): lax.ppermute(down, axis, [((i + 1) % count, i) for i in range(count)])]
  transfers between devices with their start and end apart: 6 -> 6, of which waited for: 4 -> 3; matrix products, arithmetic and copies ran while one was open for 1% -> 2% of each run, Pallas kernels for 3% -> 2%
where the time goes in v2:
time: 87.9 us; the launch traced here: 87.4 us
  blocking collectives  38.5 us (44%)
  starting transfers between devices  29.4 us (33%)
  Pallas kernels  12 us (14%)
  local copies, waits for them, and re-layouts  3.68 us (4%)
  waiting for transfers between devices  3.19 us (4%)
    ppermute x3, starting transfers between devices, swapped(): lax.ppermute(down, axis, [((i + 1) % count, i) for i in range(count)])  25.5 us
    all_to_all x1, blocking collectives, shards(): column = lax.all_to_all(force, ('gx_1', 'gy_1', 'gz'), 0, 0, tiled=True)  19.3 us
    all_to_all x1, blocking collectives, shards(): rows = lax.all_to_all(rows, ('gx_0', 'gy_0'), 0, 0, tiled=True)  19.2 us
    pallas_call x7, Pallas kernels, call(): pl.pallas_call(kernel, out_shape=[(pltpu.VMEM if keep else jax.ShapeDtype...  12 us
    ppermute x3, starting transfers between devices, swapped(): lax.ppermute(up, axis, [(i, (i + 1) % count) for i in range(count)])  3.84 us
    ppermute x3, waiting for transfers between devices, swapped(): lax.ppermute(down, axis, [((i + 1) % count, i) for i in range(count)])  2.82 us
    unnamed x4, local copies, waits for them, and re-layouts  1.87 us
  transfers between devices with their start and end apart: 6, of which 3 were waited for; matrix products, arithmetic and copies ran while one was open for 2% of the time, Pallas kernels for 2%

profile of v2, /device:TPU:1, one launch (start us, length us, event | category | flops | bytes accessed | tf_op | source)
XLA Modules:
  0.0 87.4 jit_solution(9318618542225173961)
XLA Ops:
  0.6 0.0 copy-start
  0.6 1.0 %copy-done = f32[19,4,8,128]{3,2,1,0:T(8,128)S(1)} copy-done((f32[19,4,8,128]{3,2,1,0:T(8,128)S(1)}, f32[19,4,8,128]{3,2,1,0:T(8,128)}, u32[]{:S(2)}) %copy-start) | copy-done | bytes 311320
  1.6 0.0 copy-start.1
  1.6 0.9 %copy-done.1 = f32[19,4,4,64]{3,2,1,0:T(4,128)S(1)} copy-done((f32[19,4,4,64]{3,2,1,0:T(4,128)S(1)}, f32[19,4,4,64]{3,2,1,0:T(4,128)}, u32[]{:S(2)}) %copy-start.1) | copy-done | bytes 77848
  2.5 0.4 collide.1
  2.9 15.0 %collective-permute-start.1 = (f32[30,8,128]{2,1,0:T(8,128)S(1)}, f32[30,8,128]{2,1,0:T(8,128)S(1)}, u32[]{:S(2)}, u32[]{:S(2)}) collective-permute-start(f32[30,8,128]{2,1,0:T(8,128)S(1)} %get-tuple-element.21), channel_id=1, source_target_pairs={{64,0},{128,64},{192,128},{256,192},{320,256},{384,320},{448,384},... | collective-permute-start | bytes 368648 | tf_op jit(solution)/shard_map/ppermute | solution.py:556
  17.9 0.0 collective-permute-start
  17.9 0.8 reshape.17.velocity
  18.7 1.0 %reshape.16.centers = s32[2304]{0:T(1024)S(1)} reshape(s32[3,3,4,4,16]{4,3,2,1,0:T(4,128)} %param.6) | data formatting | bytes 18432 | tf_op jit(solution)/shard_map/reshape | solution.py:571
  19.7 2.1 %geometry.1 = (f32[8,2,2,8,128]{4,3,2,1,0:T(8,128)S(1)}, f32[3,8,2,2,8,128]{5,4,3,2,1,0:T(8,128)S(1)}) custom-call(s32[2304]{0:T(1024)S(1)} %reshape.16.centers, f32[768]{0:T(1024)S(1)} %reshape.17.velocity, f32[30,8,128]{2,1,0:T(8,128)S(1)} %get-tuple-element.20.after), custom_call_target="tpu_custom_call" | custom-call | tf_op jit(solution)/shard_map/geometry/pallas_call | solution.py:542
  21.8 0.0 collective-permute-done.1.r_r
  21.8 0.0 collective-permute-done.r_l
  21.8 0.2 pack_y.1
  22.0 1.9 %collective-permute-start.2 = (f32[31,8,128]{2,1,0:T(8,128)S(1)}, f32[31,8,128]{2,1,0:T(8,128)S(1)}, u32[]{:S(2)}, u32[]{:S(2)}) collective-permute-start(f32[31,8,128]{2,1,0:T(8,128)S(1)} %get-tuple-element.23), channel_id=1, source_target_pairs={{0,8},{8,16},{16,24},{24,32},{32,40},{40,48},{48,56},{56,0},{1,9},... | collective-permute-start | bytes 380936 | tf_op jit(solution)/shard_map/ppermute | solution.py:555
  23.9 4.6 %collective-permute-start.3 = (f32[31,8,128]{2,1,0:T(8,128)S(1)}, f32[31,8,128]{2,1,0:T(8,128)S(1)}, u32[]{:S(2)}, u32[]{:S(2)}) collective-permute-start(f32[31,8,128]{2,1,0:T(8,128)S(1)} %get-tuple-element.24), channel_id=1, source_target_pairs={{8,0},{16,8},{24,16},{32,24},{40,32},{48,40},{56,48},{0,56},{9,1},... | collective-permute-start | bytes 380936 | tf_op jit(solution)/shard_map/ppermute | solution.py:556
  28.5 0.4 collective-permute-done.2.y_l
  28.9 1.5 %collective-permute-done.3.y_r = f32[31,8,128]{2,1,0:T(8,128)S(1)} collective-permute-done((f32[31,8,128]{2,1,0:T(8,128)S(1)}, f32[31,8,128]{2,1,0:T(8,128)S(1)}, u32[]{:S(2)}, u32[]{:S(2)}) %collective-permute-start.3) | collective-permute-done | bytes 127008 | tf_op jit(solution)/shard_map/ppermute | solution.py:556
  30.4 1.3 %pack_z.1 = (f32[20,8,16,128]{3,2,1,0:T(8,128)S(1)}, f32[19,6,8,128]{3,2,1,0:T(8,128)S(1)}, f32[8,16,128]{2,1,0:T(8,128)S(1)}, f32[8,16,128]{2,1,0:T(8,128)S(1)}) custom-call(f32[20,4,8,128]{3,2,1,0:T(8,128)S(1)} %get-tuple-element.18.fp, f32[19,4,8,128]{3,2,1,0:T(8,128)S(1)} %get-tuple-element.19.cp, f32[30,8,128]{2,1,0:T(8,128)S(1)} %collective-permute-done.r_l, ...), custom_call_target="tpu_custom_call" | custom-call | tf_op jit(solution)/shard_map/pack_z/pallas_call | solution.py:542
  31.7 1.9 %collective-permute-start.4 = (f32[8,16,128]{2,1,0:T(8,128)S(1)}, f32[8,16,128]{2,1,0:T(8,128)S(1)}, u32[]{:S(2)}, u32[]{:S(2)}) collective-permute-start(f32[8,16,128]{2,1,0:T(8,128)S(1)} %get-tuple-element.27), channel_id=1, source_target_pairs={{0,1},{1,2},{2,3},{3,4},{4,5},{5,6},{6,7},{7,0},{8,9},{9,10},{10,1... | collective-permute-start | bytes 196616 | tf_op jit(solution)/shard_map/ppermute | solution.py:555
  33.6 6.0 %collective-permute-start.5 = (f32[8,16,128]{2,1,0:T(8,128)S(1)}, f32[8,16,128]{2,1,0:T(8,128)S(1)}, u32[]{:S(2)}, u32[]{:S(2)}) collective-permute-start(f32[8,16,128]{2,1,0:T(8,128)S(1)} %get-tuple-element.28), channel_id=1, source_target_pairs={{1,0},{2,1},{3,2},{4,3},{5,4},{6,5},{7,6},{0,7},{9,8},{10,9},{11,1... | collective-permute-start | bytes 196616 | tf_op jit(solution)/shard_map/ppermute | solution.py:556
  39.6 0.0 collective-permute-done.4.z_l
  39.6 1.3 %collective-permute-done.5.z_r = f32[8,16,128]{2,1,0:T(8,128)S(1)} collective-permute-done((f32[8,16,128]{2,1,0:T(8,128)S(1)}, f32[8,16,128]{2,1,0:T(8,128)S(1)}, u32[]{:S(2)}, u32[]{:S(2)}) %collective-permute-start.5) | collective-permute-done | bytes 65568 | tf_op jit(solution)/shard_map/ppermute | solution.py:556
  40.9 7.2 %main.1 = (f32[19,4,8,128]{3,2,1,0:T(8,128)}, f32[19,4,4,64]{3,2,1,0:T(4,128)}, f32[32,128]{1,0:T(8,128)S(1)}) custom-call(f32[20,8,16,128]{3,2,1,0:T(8,128)S(1)} %get-tuple-element.25.ext_a, f32[19,6,8,128]{3,2,1,0:T(8,128)S(1)} %get-tuple-element.26.cext, f32[8,16,128]{2,1,0:T(8,128)S(1)} %collective-permute-done.4.z_l, ...), custom_call_target="tpu_custom_call" | custom-call | tf_op jit(solution)/shard_map/main/pallas_call | solution.py:542
  48.1 19.3 %all_to_all.22 = f32[32,1,128]{2,1,0:T(1,128)S(1)} all-to-all(f32[32,1,128]{2,1,0:T(1,128)S(1)} %bitcast.11), channel_id=1, replica_groups=mesh['gx_0'=8,'gx_1'=2,'gy_0'=4,'gy_1'=2,'gz'=8] {'gx_1','gy_1','gz'}, dimensions={0} | all-to-all | bytes 32768 | tf_op jit(solution)/shard_map/all_to_all | solution.py:603
  67.4 19.2 %all_to_all.23 = f32[32,1,128]{2,1,0:T(1,128)S(1)} all-to-all(f32[32,1,128]{2,1,0:T(1,128)S(1)} %bitcast.9), channel_id=1, replica_groups=mesh['gx_0'=8,'gx_1'=2,'gy_0'=4,'gy_1'=2,'gz'=8] {'gx_0','gy_0'}, dimensions={0} | all-to-all | bytes 32768 | tf_op jit(solution)/shard_map/all_to_all | solution.py:605
  86.6 0.8 boxes.1
  (1 shorter events, 0.0 us)
Async XLA Ops:
  0.6 1.0 %copy-start = (f32[19,4,8,128]{3,2,1,0:T(8,128)S(1)}, f32[19,4,8,128]{3,2,1,0:T(8,128)}, u32[]{:S(2)}) copy-start(f32[19,4,8,128]{3,2,1,0:T(8,128)} %fine.1) | copy-start | bytes 933892
  1.6 0.9 %copy-start.1 = (f32[19,4,4,64]{3,2,1,0:T(4,128)S(1)}, f32[19,4,4,64]{3,2,1,0:T(4,128)}, u32[]{:S(2)}) copy-start(f32[19,4,4,64]{3,2,1,0:T(4,128)} %coarse.1) | copy-start | bytes 233476
  2.9 18.9 %collective-permute-start.1 = (f32[30,8,128]{2,1,0:T(8,128)S(1)}, f32[30,8,128]{2,1,0:T(8,128)S(1)}, u32[]{:S(2)}, u32[]{:S(2)}) collective-permute-start(f32[30,8,128]{2,1,0:T(8,128)S(1)} %get-tuple-element.21), channel_id=1, source_target_pairs={{64,0},{128,64},{192,128},{256,192},{320,256},{384,320},{448,384},... | collective-permute-start | bytes 368648 | tf_op jit(solution)/shard_map/ppermute | solution.py:556
  17.9 3.9 %collective-permute-start = (f32[30,8,128]{2,1,0:T(8,128)S(1)}, f32[30,8,128]{2,1,0:T(8,128)S(1)}, u32[]{:S(2)}, u32[]{:S(2)}) collective-permute-start(f32[30,8,128]{2,1,0:T(8,128)S(1)} %get-tuple-element.20.after), channel_id=1, source_target_pairs={{0,64},{64,128},{128,192},{192,256},{256,320},{320,384},{384,448},... | collective-permute-start | bytes 368648 | tf_op jit(solution)/shard_map/ppermute | solution.py:555
  22.0 6.9 %collective-permute-start.2 = (f32[31,8,128]{2,1,0:T(8,128)S(1)}, f32[31,8,128]{2,1,0:T(8,128)S(1)}, u32[]{:S(2)}, u32[]{:S(2)}) collective-permute-start(f32[31,8,128]{2,1,0:T(8,128)S(1)} %get-tuple-element.23), channel_id=1, source_target_pairs={{0,8},{8,16},{16,24},{24,32},{32,40},{40,48},{48,56},{56,0},{1,9},... | collective-permute-start | bytes 380936 | tf_op jit(solution)/shard_map/ppermute | solution.py:555
  23.9 6.5 %collective-permute-start.3 = (f32[31,8,128]{2,1,0:T(8,128)S(1)}, f32[31,8,128]{2,1,0:T(8,128)S(1)}, u32[]{:S(2)}, u32[]{:S(2)}) collective-permute-start(f32[31,8,128]{2,1,0:T(8,128)S(1)} %get-tuple-element.24), channel_id=1, source_target_pairs={{8,0},{16,8},{24,16},{32,24},{40,32},{48,40},{56,48},{0,56},{9,1},... | collective-permute-start | bytes 380936 | tf_op jit(solution)/shard_map/ppermute | solution.py:556
  31.7 7.9 %collective-permute-start.4 = (f32[8,16,128]{2,1,0:T(8,128)S(1)}, f32[8,16,128]{2,1,0:T(8,128)S(1)}, u32[]{:S(2)}, u32[]{:S(2)}) collective-permute-start(f32[8,16,128]{2,1,0:T(8,128)S(1)} %get-tuple-element.27), channel_id=1, source_target_pairs={{0,1},{1,2},{2,3},{3,4},{4,5},{5,6},{6,7},{7,0},{8,9},{9,10},{10,1... | collective-permute-start | bytes 196616 | tf_op jit(solution)/shard_map/ppermute | solution.py:555
  33.6 7.3 %collective-permute-start.5 = (f32[8,16,128]{2,1,0:T(8,128)S(1)}, f32[8,16,128]{2,1,0:T(8,128)S(1)}, u32[]{:S(2)}, u32[]{:S(2)}) collective-permute-start(f32[8,16,128]{2,1,0:T(8,128)S(1)} %get-tuple-element.28), channel_id=1, source_target_pairs={{1,0},{2,1},{3,2},{4,3},{5,4},{6,5},{7,6},{0,7},{9,8},{10,9},{11,1... | collective-permute-start | bytes 196616 | tf_op jit(solution)/shard_map/ppermute | solution.py:556

commit v3 on v2

--- a/solution.py
+++ b/solution.py
@@ -131,14 +131,21 @@
     return dot(left, dot(tiles, right))
 
 
-def collide_kernel(fine, coarse, fp, cp, xr, xl):
+def collide_kernel(fine_in, coarse_in, fp, cp, xr, xl, fine, coarse, sems):
+    bring_coarse = pltpu.make_async_copy(coarse_in, coarse, sems.at[0])
+    bring_fine = pltpu.make_async_copy(fine_in, fine, sems.at[1])
+    bring_fine.start()
+    bring_coarse.start()
     gx = lax.axis_index(GX)
     last = lax.axis_size(GX) - 1
     cp[...] = jnp.zeros(cp.shape, F32)
+    bring_coarse.wait()
     for x in range(4):
         post, density = collided([coarse[q, x] for q in range(19)], COARSE_RATE)
         for q in range(19):
             cp[q, x, 0:4, 0:64] = post[q]
+
+    bring_fine.wait()
 
     def plane(x, carry):
         post, density = collided([fine[q, x] for q in range(19)], FINE_RATE)
@@ -236,14 +243,14 @@
             to_r = jnp.zeros((8, 128), F32)
             to_l = jnp.zeros((8, 128), F32)
             for f in range(20):
-                turned = pltpu.roll(ext[f, j, 8 * h : 8 * h + 8], (2 * f + 2) % 128, 1)
-                to_r = jnp.where((lane >> 1) == f, turned, to_r)
-                to_l = jnp.where((lane >> 1) == f + 1, turned, to_l)
+                turned = pltpu.roll(ext[f, j, 8 * h : 8 * h + 8], (4 * f + 2) % 128, 1)
+                to_r = jnp.where((lane >> 1) == 2 * f, turned, to_r)
+                to_l = jnp.where((lane >> 1) == 2 * f + 1, turned, to_l)
             if h == 0:
                 jc = jnp.minimum(j, 5)
                 for k in range(5):
-                    to_r = jnp.where(lane == 64 + k, pltpu.roll(cext[ZP[k], jc], k + 1, 1), to_r)
-                    to_l = jnp.where(lane == 64 + k, pltpu.roll(cext[ZM[k], jc], 64 + k, 1), to_l)
+                    to_r = jnp.where(lane == 96 + k, pltpu.roll(cext[ZP[k], jc], 33 + k, 1), to_r)
+                    to_l = jnp.where(lane == 96 + k, pltpu.roll(cext[ZM[k], jc], 96 + k, 1), to_l)
             zr[j, 8 * h : 8 * h + 8] = to_r
             zl[j, 8 * h : 8 * h + 8] = to_l
         return carry
@@ -342,7 +349,7 @@
         q = ZP[k]
         for x in range(4):
             j = 1 + x - VELOCITIES[q][0]
-            tile = jnp.where(lane == 127, pltpu.roll(z_l[j, 0:8], 63 - k, 1), cext[q, j])
+            tile = jnp.where(lane == 127, pltpu.roll(z_l[j, 0:8], 31 - k, 1), cext[q, j])
             tile = pltpu.roll(tile, 1, 1)
             if VELOCITIES[q][1]:
                 tile = pltpu.roll(tile, VELOCITIES[q][1] % 8, 0)
@@ -350,9 +357,7 @@
         q = ZM[k]
         for x in range(4):
             j = 1 + x - VELOCITIES[q][0]
-            tile = z_r[j, 0:8]
-            if k:
-                tile = pltpu.roll(tile, 128 - k, 1)
+            tile = pltpu.roll(z_r[j, 0:8], 96 - k, 1)
             tile = jnp.where(lane == 64, tile, cext[q, j])
             tile = pltpu.roll(tile, 127, 1)
             if VELOCITIES[q][1]:
@@ -370,10 +375,9 @@
         for h in range(2):
             from_l = z_l[j, 8 * h : 8 * h + 8]
             from_r = z_r[j, 8 * h : 8 * h + 8]
+            both = jnp.where((lane & 2) == 0, from_l, from_r)
             for f in range(20):
-                before = pltpu.roll(from_l, (126 - 2 * f) % 128, 1)
-                after = pltpu.roll(from_r, (126 - 2 * f) % 128, 1)
-                ext_b[f, j, 8 * h : 8 * h + 8] = jnp.where(lane < 64, after, before)
+                ext_b[f, j, 8 * h : 8 * h + 8] = pltpu.roll(both, (126 - 4 * f) % 128, 1)
         return carry
 
     lax.fori_loop(0, 8, unpack, 0)
@@ -489,15 +493,16 @@
 
     first = substep(get_first, 1, 2, 1, 7, store_first, (0, 1))
 
-    def relax(n, carry):
-        j, h, g = 1 + n // 4, (n // 2) % 2, n % 2
-        out, density = collided([post[q, j, h, g] for q in range(19)], FINE_RATE)
-        for q in range(19):
-            post[q, j, h, g] = out[q]
-        post[RHO, j, h, g] = density
+    def relax(j, carry):
+        for h in range(2):
+            for g in range(2):
+                out, density = collided([post[q, j, h, g] for q in range(19)], FINE_RATE)
+                for q in range(19):
+                    post[q, j, h, g] = out[q]
+                post[RHO, j, h, g] = density
         return carry
 
-    lax.fori_loop(0, 24, relax, 0)
+    lax.fori_loop(1, 7, relax, 0)
     for edge, j in ((0, 1), (last, 6)):
 
         @pl.when(gx == edge)
@@ -561,8 +566,14 @@
     fp, cp, xr, xl = call(
         collide_kernel,
         ((20, 4, 8, 128), (19, 4, 8, 128), (30, 8, 128), (30, 8, 128)),
-        (fine_pdfs, coarse_pdfs),
+        [pltpu.with_memory_space_constraint(x, pltpu.HBM) for x in (fine_pdfs, coarse_pdfs)],
+        specs=[ANY, ANY],
         near=[False] * 2,
+        scratch=(
+            pltpu.VMEM(fine_pdfs.shape, F32),
+            pltpu.VMEM(coarse_pdfs.shape, F32),
+            pltpu.SemaphoreType.DMA((2,)),
+        ),
         name="collide",
     )
     code, wind = call(

time: 87.9 us -> 85.9 us (0.977)
  local copies, waits for them, and re-layouts: 3.68 us -> 1.81 us
    unnamed x4 -> x0, local copies, waits for them, and re-layouts: 1.87 us -> none
where the time goes in v3:
time: 85.9 us; the launch traced here: 85.5 us
  blocking collectives  38.5 us (45%)
  starting transfers between devices  29.4 us (34%)
  Pallas kernels  11.9 us (14%)
  waiting for transfers between devices  3.19 us (4%)
  local copies, waits for them, and re-layouts  1.81 us (2%)
    ppermute x3, starting transfers between devices, swapped(): lax.ppermute(down, axis, [((i + 1) % count, i) for i in range(count)])  25.5 us
    all_to_all x1, blocking collectives, shards(): column = lax.all_to_all(force, ('gx_1', 'gy_1', 'gz'), 0, 0, tiled=True)  19.3 us
    all_to_all x1, blocking collectives, shards(): rows = lax.all_to_all(rows, ('gx_0', 'gy_0'), 0, 0, tiled=True)  19.2 us
    pallas_call x7, Pallas kernels, call(): pl.pallas_call(kernel, out_shape=[(pltpu.VMEM if keep else jax.ShapeDtype...  11.9 us
    ppermute x3, starting transfers between devices, swapped(): lax.ppermute(up, axis, [(i, (i + 1) % count) for i in range(count)])  3.84 us
    ppermute x3, waiting for transfers between devices, swapped(): lax.ppermute(down, axis, [((i + 1) % count, i) for i in range(count)])  2.82 us
  transfers between devices with their start and end apart: 6, of which 3 were waited for; matrix products, arithmetic and copies ran while one was open for 2% of the time, Pallas kernels for 2%

profile of v3, /device:TPU:1, one launch (start us, length us, event | category | flops | bytes accessed | tf_op | source)
XLA Modules:
  0.0 85.5 jit_solution(4579405687435313626)
XLA Ops:
  0.6 1.4 %collide.1 = (f32[20,4,8,128]{3,2,1,0:T(8,128)S(1)}, f32[19,4,8,128]{3,2,1,0:T(8,128)S(1)}, f32[30,8,128]{2,1,0:T(8,128)S(1)}, f32[30,8,128]{2,1,0:T(8,128)S(1)}) custom-call(f32[19,4,8,128]{3,2,1,0:T(8,128)} %fine_in.1, f32[19,4,4,64]{3,2,1,0:T(4,128)} %coarse_in.1), custom_call_target="tpu_custom_call" | custom-call | tf_op jit(solution)/shard_map/collide/pallas_call | solution.py:547
  2.0 15.0 %collective-permute-start.1 = (f32[30,8,128]{2,1,0:T(8,128)S(1)}, f32[30,8,128]{2,1,0:T(8,128)S(1)}, u32[]{:S(2)}, u32[]{:S(2)}) collective-permute-start(f32[30,8,128]{2,1,0:T(8,128)S(1)} %get-tuple-element.21), channel_id=1, source_target_pairs={{64,0},{128,64},{192,128},{256,192},{320,256},{384,320},{448,384},... | collective-permute-start | bytes 368648 | tf_op jit(solution)/shard_map/ppermute | solution.py:561
  17.1 0.0 collective-permute-start
  17.1 0.8 reshape.17.velocity
  17.9 1.0 %reshape.16.centers = s32[2304]{0:T(1024)S(1)} reshape(s32[3,3,4,4,16]{4,3,2,1,0:T(4,128)} %param.6) | data formatting | bytes 18432 | tf_op jit(solution)/shard_map/reshape | solution.py:582
  18.9 2.1 %geometry.1 = (f32[8,2,2,8,128]{4,3,2,1,0:T(8,128)S(1)}, f32[3,8,2,2,8,128]{5,4,3,2,1,0:T(8,128)S(1)}) custom-call(s32[2304]{0:T(1024)S(1)} %reshape.16.centers, f32[768]{0:T(1024)S(1)} %reshape.17.velocity, f32[30,8,128]{2,1,0:T(8,128)S(1)} %get-tuple-element.20.after), custom_call_target="tpu_custom_call" | custom-call | tf_op jit(solution)/shard_map/geometry/pallas_call | solution.py:547
  20.9 0.0 collective-permute-done.1.r_r
  21.0 0.0 collective-permute-done.r_l
  21.0 0.2 pack_y.1
  21.1 1.9 %collective-permute-start.2 = (f32[31,8,128]{2,1,0:T(8,128)S(1)}, f32[31,8,128]{2,1,0:T(8,128)S(1)}, u32[]{:S(2)}, u32[]{:S(2)}) collective-permute-start(f32[31,8,128]{2,1,0:T(8,128)S(1)} %get-tuple-element.23), channel_id=1, source_target_pairs={{0,8},{8,16},{16,24},{24,32},{32,40},{40,48},{48,56},{56,0},{1,9},... | collective-permute-start | bytes 380936 | tf_op jit(solution)/shard_map/ppermute | solution.py:560
  23.1 4.6 %collective-permute-start.3 = (f32[31,8,128]{2,1,0:T(8,128)S(1)}, f32[31,8,128]{2,1,0:T(8,128)S(1)}, u32[]{:S(2)}, u32[]{:S(2)}) collective-permute-start(f32[31,8,128]{2,1,0:T(8,128)S(1)} %get-tuple-element.24), channel_id=1, source_target_pairs={{8,0},{16,8},{24,16},{32,24},{40,32},{48,40},{56,48},{0,56},{9,1},... | collective-permute-start | bytes 380936 | tf_op jit(solution)/shard_map/ppermute | solution.py:561
  27.6 0.4 collective-permute-done.2.y_l
  28.0 1.5 %collective-permute-done.3.y_r = f32[31,8,128]{2,1,0:T(8,128)S(1)} collective-permute-done((f32[31,8,128]{2,1,0:T(8,128)S(1)}, f32[31,8,128]{2,1,0:T(8,128)S(1)}, u32[]{:S(2)}, u32[]{:S(2)}) %collective-permute-start.3) | collective-permute-done | bytes 127008 | tf_op jit(solution)/shard_map/ppermute | solution.py:561
  29.5 1.3 %pack_z.1 = (f32[20,8,16,128]{3,2,1,0:T(8,128)S(1)}, f32[19,6,8,128]{3,2,1,0:T(8,128)S(1)}, f32[8,16,128]{2,1,0:T(8,128)S(1)}, f32[8,16,128]{2,1,0:T(8,128)S(1)}) custom-call(f32[20,4,8,128]{3,2,1,0:T(8,128)S(1)} %get-tuple-element.18.fp, f32[19,4,8,128]{3,2,1,0:T(8,128)S(1)} %get-tuple-element.19.cp, f32[30,8,128]{2,1,0:T(8,128)S(1)} %collective-permute-done.r_l, ...), custom_call_target="tpu_custom_call" | custom-call | tf_op jit(solution)/shard_map/pack_z/pallas_call | solution.py:547
  30.8 1.9 %collective-permute-start.4 = (f32[8,16,128]{2,1,0:T(8,128)S(1)}, f32[8,16,128]{2,1,0:T(8,128)S(1)}, u32[]{:S(2)}, u32[]{:S(2)}) collective-permute-start(f32[8,16,128]{2,1,0:T(8,128)S(1)} %get-tuple-element.27), channel_id=1, source_target_pairs={{0,1},{1,2},{2,3},{3,4},{4,5},{5,6},{6,7},{7,0},{8,9},{9,10},{10,1... | collective-permute-start | bytes 196616 | tf_op jit(solution)/shard_map/ppermute | solution.py:560
  32.8 5.9 %collective-permute-start.5 = (f32[8,16,128]{2,1,0:T(8,128)S(1)}, f32[8,16,128]{2,1,0:T(8,128)S(1)}, u32[]{:S(2)}, u32[]{:S(2)}) collective-permute-start(f32[8,16,128]{2,1,0:T(8,128)S(1)} %get-tuple-element.28), channel_id=1, source_target_pairs={{1,0},{2,1},{3,2},{4,3},{5,4},{6,5},{7,6},{0,7},{9,8},{10,9},{11,1... | collective-permute-start | bytes 196616 | tf_op jit(solution)/shard_map/ppermute | solution.py:561
  38.7 0.0 collective-permute-done.4.z_l
  38.7 1.3 %collective-permute-done.5.z_r = f32[8,16,128]{2,1,0:T(8,128)S(1)} collective-permute-done((f32[8,16,128]{2,1,0:T(8,128)S(1)}, f32[8,16,128]{2,1,0:T(8,128)S(1)}, u32[]{:S(2)}, u32[]{:S(2)}) %collective-permute-start.5) | collective-permute-done | bytes 65568 | tf_op jit(solution)/shard_map/ppermute | solution.py:561
  40.0 6.2 %main.1 = (f32[19,4,8,128]{3,2,1,0:T(8,128)}, f32[19,4,4,64]{3,2,1,0:T(4,128)}, f32[32,128]{1,0:T(8,128)S(1)}) custom-call(f32[20,8,16,128]{3,2,1,0:T(8,128)S(1)} %get-tuple-element.25.ext_a, f32[19,6,8,128]{3,2,1,0:T(8,128)S(1)} %get-tuple-element.26.cext, f32[8,16,128]{2,1,0:T(8,128)S(1)} %collective-permute-done.4.z_l, ...), custom_call_target="tpu_custom_call" | custom-call | tf_op jit(solution)/shard_map/main/pallas_call | solution.py:547
  46.2 19.3 %all_to_all.22 = f32[32,1,128]{2,1,0:T(1,128)S(1)} all-to-all(f32[32,1,128]{2,1,0:T(1,128)S(1)} %bitcast.11), channel_id=1, replica_groups=mesh['gx_0'=8,'gx_1'=2,'gy_0'=4,'gy_1'=2,'gz'=8] {'gx_1','gy_1','gz'}, dimensions={0} | all-to-all | bytes 32768 | tf_op jit(solution)/shard_map/all_to_all | solution.py:614
  65.5 19.2 %all_to_all.23 = f32[32,1,128]{2,1,0:T(1,128)S(1)} all-to-all(f32[32,1,128]{2,1,0:T(1,128)S(1)} %bitcast.9), channel_id=1, replica_groups=mesh['gx_0'=8,'gx_1'=2,'gy_0'=4,'gy_1'=2,'gz'=8] {'gx_0','gy_0'}, dimensions={0} | all-to-all | bytes 32768 | tf_op jit(solution)/shard_map/all_to_all | solution.py:616
  84.7 0.8 boxes.1
  (1 shorter events, 0.0 us)
Async XLA Ops:
  2.0 18.9 %collective-permute-start.1 = (f32[30,8,128]{2,1,0:T(8,128)S(1)}, f32[30,8,128]{2,1,0:T(8,128)S(1)}, u32[]{:S(2)}, u32[]{:S(2)}) collective-permute-start(f32[30,8,128]{2,1,0:T(8,128)S(1)} %get-tuple-element.21), channel_id=1, source_target_pairs={{64,0},{128,64},{192,128},{256,192},{320,256},{384,320},{448,384},... | collective-permute-start | bytes 368648 | tf_op jit(solution)/shard_map/ppermute | solution.py:561
  17.1 3.9 %collective-permute-start = (f32[30,8,128]{2,1,0:T(8,128)S(1)}, f32[30,8,128]{2,1,0:T(8,128)S(1)}, u32[]{:S(2)}, u32[]{:S(2)}) collective-permute-start(f32[30,8,128]{2,1,0:T(8,128)S(1)} %get-tuple-element.20.after), channel_id=1, source_target_pairs={{0,64},{64,128},{128,192},{192,256},{256,320},{320,384},{384,448},... | collective-permute-start | bytes 368648 | tf_op jit(solution)/shard_map/ppermute | solution.py:560
  21.1 6.9 %collective-permute-start.2 = (f32[31,8,128]{2,1,0:T(8,128)S(1)}, f32[31,8,128]{2,1,0:T(8,128)S(1)}, u32[]{:S(2)}, u32[]{:S(2)}) collective-permute-start(f32[31,8,128]{2,1,0:T(8,128)S(1)} %get-tuple-element.23), channel_id=1, source_target_pairs={{0,8},{8,16},{16,24},{24,32},{32,40},{40,48},{48,56},{56,0},{1,9},... | collective-permute-start | bytes 380936 | tf_op jit(solution)/shard_map/ppermute | solution.py:560
  23.1 6.5 %collective-permute-start.3 = (f32[31,8,128]{2,1,0:T(8,128)S(1)}, f32[31,8,128]{2,1,0:T(8,128)S(1)}, u32[]{:S(2)}, u32[]{:S(2)}) collective-permute-start(f32[31,8,128]{2,1,0:T(8,128)S(1)} %get-tuple-element.24), channel_id=1, source_target_pairs={{8,0},{16,8},{24,16},{32,24},{40,32},{48,40},{56,48},{0,56},{9,1},... | collective-permute-start | bytes 380936 | tf_op jit(solution)/shard_map/ppermute | solution.py:561
  30.8 7.9 %collective-permute-start.4 = (f32[8,16,128]{2,1,0:T(8,128)S(1)}, f32[8,16,128]{2,1,0:T(8,128)S(1)}, u32[]{:S(2)}, u32[]{:S(2)}) collective-permute-start(f32[8,16,128]{2,1,0:T(8,128)S(1)} %get-tuple-element.27), channel_id=1, source_target_pairs={{0,1},{1,2},{2,3},{3,4},{4,5},{5,6},{6,7},{7,0},{8,9},{9,10},{10,1... | collective-permute-start | bytes 196616 | tf_op jit(solution)/shard_map/ppermute | solution.py:560
  32.8 7.3 %collective-permute-start.5 = (f32[8,16,128]{2,1,0:T(8,128)S(1)}, f32[8,16,128]{2,1,0:T(8,128)S(1)}, u32[]{:S(2)}, u32[]{:S(2)}) collective-permute-start(f32[8,16,128]{2,1,0:T(8,128)S(1)} %get-tuple-element.28), channel_id=1, source_target_pairs={{1,0},{2,1},{3,2},{4,3},{5,4},{6,5},{7,6},{0,7},{9,8},{10,9},{11,1... | collective-permute-start | bytes 196616 | tf_op jit(solution)/shard_map/ppermute | solution.py:561
